TPU v7x, 64 devices: a 2x2x8 block of a 4x4x8 slice. The times are simulated.
64 devices in a mesh: videos: 4 (over x, y), frames: 16 (over z, core).
Axes of the slice: x: 2, y: 2, z: 8, core: 2. Of those that a mesh axis runs over, the one named last changes fastest.
The devices are a block of a 4x4x8 slice.
Arguments:
- latents_a: float32 [1024, 256, 4], P(('videos', 'frames')), parts along dimension 0
- mod_a: float32 [1024, 1, 6, 384], P(('videos', 'frames')), parts along dimension 0
- dt_a: float32 [1024], P(('videos', 'frames')), parts along dimension 0
- noise_a: float32 [12, 256, 4], P('videos'), parts along dimension 0
- latents_b: float32 [1024, 256, 4], P(('videos', 'frames')), parts along dimension 0
- mod_b: float32 [1024, 1, 6, 384], P(('videos', 'frames')), parts along dimension 0
- dt_b: float32 [1024], P(('videos', 'frames')), parts along dimension 0
- noise_b: float32 [12, 256, 4], P('videos'), parts along dimension 0
- w_in: bfloat16 [4, 384], replicated
- sp_qkv: bfloat16 [1, 384, 3, 6, 64], replicated
- sp_out: bfloat16 [1, 6, 64, 384], replicated
- tm_qkv: bfloat16 [1, 384, 3, 6, 64], replicated
- tm_bias: float32 [1, 6, 16], replicated
- tm_out: bfloat16 [1, 6, 64, 384], replicated
- mlp_up: bfloat16 [1, 384, 1536], replicated
- mlp_down: bfloat16 [1, 1536, 384], replicated
- w_out: bfloat16 [384, 4], replicated
Outputs:
- output 1: float32 [12, 256, 4], P('videos', 'frames'), parts along dimension 0
- output 2: float32 [1024, 256, 4], P(('videos', 'frames')), parts along dimension 0
- output 3: float32 [12, 256, 4], P('videos', 'frames'), parts along dimension 0
- output 4: float32 [1024, 256, 4], P(('videos', 'frames')), parts along dimension 0
There are 4 independent parts. A program takes and returns all parts, laid end to end along the dimension named above; an argument that names none is the same for every part.
All inputs are finite; a program needn't handle non-finite values.
Results may differ from a plain program's by a relative error of at most 0.0112564.
Values are sent between devices in bfloat16 or wider.
A program may use at most 768 MiB of HBM per device.

v0:
```python
import jax
import jax.numpy as jnp
from jax import lax
from jax.sharding import PartitionSpec as P, NamedSharding

LN_EPS = 1e-6
MASKED = -1e30


def layer_norm(hidden):
    values = hidden.astype(jnp.float32)
    centered = values - jnp.mean(values, axis=-1, keepdims=True)
    variance = jnp.mean(centered * centered, axis=-1, keepdims=True)
    return centered * lax.rsqrt(variance + LN_EPS)


def modulate(hidden, mod_layer, pair):
    shift = mod_layer[..., 2 * pair:2 * pair + 1, :]
    scale = mod_layer[..., 2 * pair + 1:2 * pair + 2, :]
    return (layer_norm(hidden) * (1.0 + scale) + shift).astype(jnp.bfloat16)


def add_residual(hidden, delta):
    return (hidden.astype(jnp.float32) + delta).astype(jnp.bfloat16)


def project_qkv(normed, w_qkv):
    return jnp.einsum('...d,dshe->...she', normed, w_qkv, preferred_element_type=jnp.float32).astype(jnp.bfloat16)


def spatial_mix(normed, w_qkv, w_proj):
    projected = project_qkv(normed, w_qkv)
    scores = jnp.einsum('...qhe,...khe->...hqk', projected[..., 0, :, :], projected[..., 1, :, :], preferred_element_type=jnp.float32) * projected.shape[-1] ** -0.5
    attn_probs = jax.nn.softmax(scores, axis=-1).astype(jnp.bfloat16)
    mixed = jnp.einsum('...hqk,...khe->...qhe', attn_probs, projected[..., 2, :, :], preferred_element_type=jnp.float32).astype(jnp.bfloat16)
    return jnp.einsum('...qhe,hed->...qd', mixed, w_proj, preferred_element_type=jnp.float32)


def band_bias(bias_layer, frames_local, first_block):
    window = bias_layer.shape[-1]
    span = frames_local + window - 1
    key_pos = jnp.arange(span)
    offset = jnp.arange(frames_local)[:, None] + (window - 1) - key_pos[None, :]
    inside = (offset >= 0) & (offset < window)
    from_halo = key_pos < window - 1
    keep = inside & jnp.logical_not(from_halo & first_block[..., None, None])
    table = jnp.take(bias_layer, jnp.clip(offset, 0, window - 1), axis=-1)
    return jnp.where(keep[..., None, :, :], table, MASKED)


def temporal_mix(projected, halo, w_proj, band):
    keys_all = jnp.concatenate([halo[..., 0, :, :], projected[..., 1, :, :]], axis=-4)
    values_all = jnp.concatenate([halo[..., 1, :, :], projected[..., 2, :, :]], axis=-4)
    scores = jnp.einsum('...fphe,...jphe->...phfj', projected[..., 0, :, :], keys_all, preferred_element_type=jnp.float32)
    scores = scores * projected.shape[-1] ** -0.5 + band[..., None, :, :, :]
    attn_probs = jax.nn.softmax(scores, axis=-1).astype(jnp.bfloat16)
    mixed = jnp.einsum('...phfj,...jphe->...fphe', attn_probs, values_all, preferred_element_type=jnp.float32).astype(jnp.bfloat16)
    return jnp.einsum('...fphe,hed->...fpd', mixed, w_proj, preferred_element_type=jnp.float32)


def mlp_mix(normed, w_up, w_down):
    inner = jnp.einsum('...d,df->...f', normed, w_up, preferred_element_type=jnp.float32)
    activated = jax.nn.gelu(inner, approximate=True).astype(jnp.bfloat16)
    return jnp.einsum('...f,fd->...d', activated, w_down, preferred_element_type=jnp.float32)


def solution(mesh):
    group = mesh.shape['frames']
    slot_spec = P(('videos', 'frames'))
    emit_spec = P('videos', 'frames')
    whole = P()
    to_next = [(source, source + 1) for source in range(group - 1)]
    to_prev = [(source + 1, source) for source in range(group - 1)]

    def local(latents_a, mod_a, dt_a, noise_a, latents_b, mod_b, dt_b, noise_b, w_in, sp_qkv, sp_out, tm_qkv, tm_bias, tm_out, mlp_up, mlp_down, w_out):
        position = lax.axis_index('frames')
        frames_local = latents_a.shape[0]
        layers = sp_qkv.shape[0]
        halo_len = tm_bias.shape[-1] - 1
        queue = jnp.stack([latents_a, latents_b])
        modulation = jnp.stack([mod_a, mod_b])
        step_dt = jnp.stack([dt_a, dt_b])[:, :, None, None]
        noise = jnp.stack([noise_a, noise_b], axis=1)
        bands = [band_bias(tm_bias[layer], frames_local, position == 0) for layer in range(layers)]

        def step(current, noise_frame):
            hidden = jnp.einsum('...c,cd->...d', current.astype(jnp.bfloat16), w_in, preferred_element_type=jnp.float32).astype(jnp.bfloat16)
            for layer in range(layers):
                mod_layer = modulation[:, :, layer]
                hidden = add_residual(hidden, spatial_mix(modulate(hidden, mod_layer, 0), sp_qkv[layer], sp_out[layer]))
                projected = project_qkv(modulate(hidden, mod_layer, 1), tm_qkv[layer])
                halo = lax.ppermute(projected[:, frames_local - halo_len:, :, 1:], 'frames', to_next)
                hidden = add_residual(hidden, temporal_mix(projected, halo, tm_out[layer], bands[layer]))
                hidden = add_residual(hidden, mlp_mix(modulate(hidden, mod_layer, 2), mlp_up[layer], mlp_down[layer]))
            velocity = jnp.einsum('...d,dc->...c', layer_norm(hidden).astype(jnp.bfloat16), w_out, preferred_element_type=jnp.float32)
            updated = current + step_dt * velocity
            from_next = lax.ppermute(updated[:, 0], 'frames', to_prev)
            incoming = jnp.where(position == group - 1, noise_frame, from_next)
            return jnp.concatenate([updated[:, 1:], incoming[:, None]], axis=1), updated[:, 0]

        final, emitted = lax.scan(step, queue, noise)
        emitted = lax.psum_scatter(jnp.where(position == 0, emitted, 0.0), 'frames', scatter_dimension=2, tiled=True)
        return emitted[:, 0], final[0], emitted[:, 1], final[1]

    return jax.shard_map(local, mesh=mesh, in_specs=(slot_spec, slot_spec, slot_spec, P('videos'), slot_spec, slot_spec, slot_spec, P('videos')) + (whole,) * 9, out_specs=(emit_spec, slot_spec, emit_spec, slot_spec), check_vma=False)
```

profile of v0, /device:TPU:22, one launch (start us, length us, event | category | flops | bytes accessed | tf_op | source)
XLA Modules:
  0.0 1466.2 jit_solution(3807321867361753574)
XLA Ops:
  14.9 1377.9 %while.15 = (s32[]{:T(128)}, f32[2,16,256,4]{2,3,1,0:T(4,128)S(1)}, f32[3,2,256,4]{2,3,0,1:T(4,128)}, f32[2,16,1,1]{1,0,3,2:T(2,128)}, bf16[4,384]{1,0:T(4,128)(...) while((s32[]{:T(128)}, f32[2,16,256,4]{2,3,1,0:T(4,128)S(1)}, ...), condition=%wide.region_13.14_spmd.clone, body=%wide.region_0.13_spmd.sunk.clone | while | flops 42715357184 | bytes 780391808 | solution.py:101
  24.3 16.0 %convolution_convert_fusion.7 = bf16[2,16,256,3,6,64]{2,5,4,3,1,0:T(8,128)(2,1)} fusion(bf16[2,16,256,384]{3,2,1,0:T(8,128)(2,1)} %copy-done, f32[2,16,384]{2,1,0:T(8,128)S(1)} %get-tuple-element.467, f32[2,16,384]{2,1,0:T(8,128)S(1)} %get-tuple-element.468, f32[2,16,256]{2,1,0:T(8,128)S(1)} %add_rsqrt_fusion.12, ...), kind=kOutput, calls=%fused_computation.42.clone.1.clone | convolution fusion | flops 7276068864 | bytes 26214400 | tf_op jit(solution)/shard_map/while/body/eval_jaxpr/...d,dshe->...she/dot_general | solution.py:28
  40.3 25.2 %fusion.196 = (f32[2,16,6,256]{3,2,1,0:T(8,128)S(1)}, f32[2,16,6,256,256]{3,4,2,1,0:T(8,128)}) fusion(bf16[2,16,256,3,6,64]{2,5,4,3,1,0:T(8,128)(2,1)} %convolution_convert_fusion.7), kind=kOutput, calls=%fused_computation.163.clone.1.clone | convolution fusion | flops 1648361728 | bytes 63111168 | tf_op jit(solution)/shard_map/while/body/eval_jaxpr/sub | solution.py:34
  65.6 25.5 %convert_reduce_fusion.13 = (f32[2,16,256]{2,1,0:T(8,128)S(1)}, bf16[2,16,256,384]{3,2,1,0:T(8,128)(2,1)}) fusion(bf16[1,6,64,384]{3,2,1,0:T(8,128)(2,1)S(1)} %copy-done.14, f32[2,16,6,256,256]{3,4,2,1,0:T(8,128)} %get-tuple-element.470, f32[2,16,6,256]{3,2,1,0:T(8,128)S(1)} %get-tuple-element.471, ...), kind=kOutput, calls=%fused_computation.27.clone.1.clone | convolution fusion | flops 4070563840 | bytes 69730304 | tf_op jit(solution)/shard_map/while/body/eval_jaxpr/...qhe,hed->...qd/dot_general | solution.py:36
  91.1 5.1 fusion.197
  96.3 16.1 %convolution_convert_fusion.8 = bf16[2,16,256,3,6,64]{2,5,4,3,1,0:T(8,128)(2,1)} fusion(bf16[2,16,256,384]{3,2,1,0:T(8,128)(2,1)} %get-tuple-element.472, f32[2,16,384]{2,1,0:T(8,128)S(1)} %get-tuple-element.473, f32[2,16,384]{2,1,0:T(8,128)S(1)} %get-tuple-element.474, f32[2,16,256]{2,1,0:T(8,128)S(1)} %add_rsqrt_fusion.13, ...), kind=kOutput, calls=%fused_computation.41.clone.1.clone | convolution fusion | flops 7276068864 | bytes 26214400 | tf_op jit(solution)/shard_map/while/body/eval_jaxpr/...d,dshe->...she/dot_general | solution.py:28
  112.4 8.1 slice.204
  120.5 5.8 copy.94
  126.3 6.1 collective-permute-start
  132.4 8.2 slice_bitcast_fusion.56
  140.6 18.5 %copy.96 = bf16[2,16,256,6,64]{4,1,3,2,0:T(8,128)(2,1)} copy(bf16[2,16,256,6,64]{2,4,3,1,0:T(8,128)(2,1)} %get-tuple-element.481) | data formatting | bytes 12582912 | tf_op jit(solution)/shard_map/while/body/eval_jaxpr/squeeze | solution.py:54
  159.1 6.0 slice_bitcast_fusion.57
  165.4 11.1 pad_maximum_fusion.10
  176.5 35.4 %copy.97 = bf16[2,31,256,6,64]{4,1,3,2,0:T(8,128)(2,1)} copy(bf16[2,31,256,6,64]{2,4,3,1,0:T(8,128)(2,1)} %get-tuple-element.482) | data formatting | bytes 24379392 | tf_op jit(solution)/shard_map/while/body/eval_jaxpr/concatenate | solution.py:52
  211.9 35.4 %copy.95 = bf16[2,31,256,6,64]{4,1,3,2,0:T(8,128)(2,1)} copy(bf16[2,31,256,6,64]{2,4,3,1,0:T(8,128)(2,1)} %get-tuple-element.480) | data formatting | bytes 24379392 | tf_op jit(solution)/shard_map/while/body/eval_jaxpr/concatenate | solution.py:53
  247.3 28.3 %fusion.198 = (f32[2,256,6,16]{3,2,1,0:T(8,128)S(1)}, f32[2,256,6,16,31]{4,3,2,1,0:T(8,128)}) fusion(f32[6,16,31]{2,1,0:T(8,128)S(1)} %copy-done.2, bf16[2,16,256,6,64]{4,1,3,2,0:T(8,128)(2,1)} %copy.96, bf16[2,31,256,6,64]{4,1,3,2,0:T(8,128)(2,1)} %copy.97), kind=kOutput, calls=%fused_computation.164.clone.1.clone | convolution fusion | flops 201130016 | bytes 24784512 | tf_op jit(solution)/shard_map/while/body/eval_jaxpr/sub | solution.py:56
  275.6 22.4 %convert_bitcast_fusion.3 = bf16[2,16,256,6,64]{4,1,3,2,0:T(8,128)(2,1)} fusion(bf16[2,31,256,6,64]{4,1,3,2,0:T(8,128)(2,1)} %copy.95, f32[2,256,6,16,31]{4,3,2,1,0:T(8,128)} %get-tuple-element.483, f32[2,256,6,16]{3,2,1,0:T(8,128)S(1)} %get-tuple-element.484), kind=kOutput, calls=%fused_computation.64.clone.1.clone | convolution fusion | flops 201228288 | bytes 24772608 | tf_op jit(solution)/shard_map/while/body/eval_jaxpr/...phfj,...jphe->...fphe/dot_general | solution.py:57
  298.0 16.9 %convert_reduce_fusion.14 = (f32[2,16,256]{2,1,0:T(8,128)S(1)}, bf16[2,16,256,384]{3,2,1,0:T(8,128)(2,1)S(1)}) fusion(bf16[1,6,64,384]{3,2,1,0:T(8,128)(2,1)S(1)} %copy-done.15, bf16[2,16,256,6,64]{4,1,3,2,0:T(8,128)(2,1)} %convert_bitcast_fusion.3, bf16[2,16,256,384]{3,2,1,0:T(8,128)(2,1)} %get-tuple-element.472), kind=kOutput, calls=%fused_computation.24.clone.1.clone | convolution fusion | flops 2431639552 | bytes 19202048 | tf_op jit(solution)/shard_map/while/body/eval_jaxpr/...fphe,hed->...fpd/dot_general | solution.py:58
  318.0 23.3 %fusion.9.clone.3.clone.7 = bf16[2,16,256,1536]{3,2,1,0:T(8,128)(2,1)} fusion(bf16[2,16,256,384]{3,2,1,0:T(8,128)(2,1)S(1)} %get-tuple-element.485, f32[2,16,384]{2,1,0:T(8,128)S(1)} %copy-done.8, f32[2,16,384]{2,1,0:T(8,128)S(1)} %copy-done.7, f32[2,16,256]{2,1,0:T(8,128)S(1)} %add_rsqrt_fusion.14, ...), kind=kOutput, calls=%fused_computation.11.clone.clone.clone.clone.clone.clone.clone.1.clone.1.clone | convolution fusion | flops 9795796992 | bytes 32800768 | tf_op jit(solution)/shard_map/while/body/eval_jaxpr/...d,df->...f/dot_general | solution.py:62
  341.3 21.0 %convert_reduce_fusion.15 = (f32[2,16,256]{2,1,0:T(8,128)S(1)}, bf16[2,16,256,384]{3,2,1,0:T(8,128)(2,1)}) fusion(bf16[1,1536,384]{2,1,0:T(8,128)(2,1)S(1)} %copy-done.11, bf16[2,16,256,384]{3,2,1,0:T(8,128)(2,1)} %copy-done.1, bf16[2,16,256,1536]{3,2,1,0:T(8,128)(2,1)} %fusion.9.clone.3.clone.7), kind=kOutput, calls=%fused_computation.32.clone.2.clone | convolution fusion | flops 9679396864 | bytes 38961152 | tf_op jit(solution)/shard_map/while/body/eval_jaxpr/...f,fd->...d/dot_general | solution.py:64
  362.4 5.2 fusion.200
  374.1 97.7 %collective-permute-done.1 = f32[2,256,4]{1,2,0:T(4,128)S(1)} collective-permute-done((f32[2,256,4]{1,2,0:T(4,128)S(1)}, f32[2,256,4]{1,2,0:T(4,128)S(1)}, u32[]{:S(2)}, u32[]{:S(2)}) %collective-permute-start.1) | collective-permute-done | bytes 8224 | tf_op jit(solution)/shard_map/while/body/eval_jaxpr/ppermute | solution.py:97
  482.4 16.0 %convolution_convert_fusion.7 = bf16[2,16,256,3,6,64]{2,5,4,3,1,0:T(8,128)(2,1)} fusion(bf16[2,16,256,384]{3,2,1,0:T(8,128)(2,1)} %copy-done, f32[2,16,384]{2,1,0:T(8,128)S(1)} %get-tuple-element.467, f32[2,16,384]{2,1,0:T(8,128)S(1)} %get-tuple-element.468, f32[2,16,256]{2,1,0:T(8,128)S(1)} %add_rsqrt_fusion.12, ...), kind=kOutput, calls=%fused_computation.42.clone.1.clone | convolution fusion | flops 7276068864 | bytes 26214400 | tf_op jit(solution)/shard_map/while/body/eval_jaxpr/...d,dshe->...she/dot_general | solution.py:28
  498.4 25.2 %fusion.196 = (f32[2,16,6,256]{3,2,1,0:T(8,128)S(1)}, f32[2,16,6,256,256]{3,4,2,1,0:T(8,128)}) fusion(bf16[2,16,256,3,6,64]{2,5,4,3,1,0:T(8,128)(2,1)} %convolution_convert_fusion.7), kind=kOutput, calls=%fused_computation.163.clone.1.clone | convolution fusion | flops 1648361728 | bytes 63111168 | tf_op jit(solution)/shard_map/while/body/eval_jaxpr/sub | solution.py:34
  523.7 25.5 %convert_reduce_fusion.13 = (f32[2,16,256]{2,1,0:T(8,128)S(1)}, bf16[2,16,256,384]{3,2,1,0:T(8,128)(2,1)}) fusion(bf16[1,6,64,384]{3,2,1,0:T(8,128)(2,1)S(1)} %copy-done.14, f32[2,16,6,256,256]{3,4,2,1,0:T(8,128)} %get-tuple-element.470, f32[2,16,6,256]{3,2,1,0:T(8,128)S(1)} %get-tuple-element.471, ...), kind=kOutput, calls=%fused_computation.27.clone.1.clone | convolution fusion | flops 4070563840 | bytes 69730304 | tf_op jit(solution)/shard_map/while/body/eval_jaxpr/...qhe,hed->...qd/dot_general | solution.py:36
  549.1 5.1 fusion.197
  554.3 16.1 %convolution_convert_fusion.8 = bf16[2,16,256,3,6,64]{2,5,4,3,1,0:T(8,128)(2,1)} fusion(bf16[2,16,256,384]{3,2,1,0:T(8,128)(2,1)} %get-tuple-element.472, f32[2,16,384]{2,1,0:T(8,128)S(1)} %get-tuple-element.473, f32[2,16,384]{2,1,0:T(8,128)S(1)} %get-tuple-element.474, f32[2,16,256]{2,1,0:T(8,128)S(1)} %add_rsqrt_fusion.13, ...), kind=kOutput, calls=%fused_computation.41.clone.1.clone | convolution fusion | flops 7276068864 | bytes 26214400 | tf_op jit(solution)/shard_map/while/body/eval_jaxpr/...d,dshe->...she/dot_general | solution.py:28
  570.4 8.1 slice.204
  578.5 5.8 copy.94
  584.3 9.4 collective-permute-start
  593.8 7.8 slice_bitcast_fusion.56
  601.6 18.5 %copy.96 = bf16[2,16,256,6,64]{4,1,3,2,0:T(8,128)(2,1)} copy(bf16[2,16,256,6,64]{2,4,3,1,0:T(8,128)(2,1)} %get-tuple-element.481) | data formatting | bytes 12582912 | tf_op jit(solution)/shard_map/while/body/eval_jaxpr/squeeze | solution.py:54
  620.1 6.0 slice_bitcast_fusion.57
  626.4 11.1 pad_maximum_fusion.10
  637.5 35.4 %copy.97 = bf16[2,31,256,6,64]{4,1,3,2,0:T(8,128)(2,1)} copy(bf16[2,31,256,6,64]{2,4,3,1,0:T(8,128)(2,1)} %get-tuple-element.482) | data formatting | bytes 24379392 | tf_op jit(solution)/shard_map/while/body/eval_jaxpr/concatenate | solution.py:52
  672.9 35.4 %copy.95 = bf16[2,31,256,6,64]{4,1,3,2,0:T(8,128)(2,1)} copy(bf16[2,31,256,6,64]{2,4,3,1,0:T(8,128)(2,1)} %get-tuple-element.480) | data formatting | bytes 24379392 | tf_op jit(solution)/shard_map/while/body/eval_jaxpr/concatenate | solution.py:53
  708.3 28.3 %fusion.198 = (f32[2,256,6,16]{3,2,1,0:T(8,128)S(1)}, f32[2,256,6,16,31]{4,3,2,1,0:T(8,128)}) fusion(f32[6,16,31]{2,1,0:T(8,128)S(1)} %copy-done.2, bf16[2,16,256,6,64]{4,1,3,2,0:T(8,128)(2,1)} %copy.96, bf16[2,31,256,6,64]{4,1,3,2,0:T(8,128)(2,1)} %copy.97), kind=kOutput, calls=%fused_computation.164.clone.1.clone | convolution fusion | flops 201130016 | bytes 24784512 | tf_op jit(solution)/shard_map/while/body/eval_jaxpr/sub | solution.py:56
  736.6 22.4 %convert_bitcast_fusion.3 = bf16[2,16,256,6,64]{4,1,3,2,0:T(8,128)(2,1)} fusion(bf16[2,31,256,6,64]{4,1,3,2,0:T(8,128)(2,1)} %copy.95, f32[2,256,6,16,31]{4,3,2,1,0:T(8,128)} %get-tuple-element.483, f32[2,256,6,16]{3,2,1,0:T(8,128)S(1)} %get-tuple-element.484), kind=kOutput, calls=%fused_computation.64.clone.1.clone | convolution fusion | flops 201228288 | bytes 24772608 | tf_op jit(solution)/shard_map/while/body/eval_jaxpr/...phfj,...jphe->...fphe/dot_general | solution.py:57
  759.0 17.0 %convert_reduce_fusion.14 = (f32[2,16,256]{2,1,0:T(8,128)S(1)}, bf16[2,16,256,384]{3,2,1,0:T(8,128)(2,1)S(1)}) fusion(bf16[1,6,64,384]{3,2,1,0:T(8,128)(2,1)S(1)} %copy-done.15, bf16[2,16,256,6,64]{4,1,3,2,0:T(8,128)(2,1)} %convert_bitcast_fusion.3, bf16[2,16,256,384]{3,2,1,0:T(8,128)(2,1)} %get-tuple-element.472), kind=kOutput, calls=%fused_computation.24.clone.1.clone | convolution fusion | flops 2431639552 | bytes 19202048 | tf_op jit(solution)/shard_map/while/body/eval_jaxpr/...fphe,hed->...fpd/dot_general | solution.py:58
  779.1 23.4 %fusion.9.clone.3.clone.7 = bf16[2,16,256,1536]{3,2,1,0:T(8,128)(2,1)} fusion(bf16[2,16,256,384]{3,2,1,0:T(8,128)(2,1)S(1)} %get-tuple-element.485, f32[2,16,384]{2,1,0:T(8,128)S(1)} %copy-done.8, f32[2,16,384]{2,1,0:T(8,128)S(1)} %copy-done.7, f32[2,16,256]{2,1,0:T(8,128)S(1)} %add_rsqrt_fusion.14, ...), kind=kOutput, calls=%fused_computation.11.clone.clone.clone.clone.clone.clone.clone.1.clone.1.clone | convolution fusion | flops 9795796992 | bytes 32800768 | tf_op jit(solution)/shard_map/while/body/eval_jaxpr/...d,df->...f/dot_general | solution.py:62
  802.5 21.0 %convert_reduce_fusion.15 = (f32[2,16,256]{2,1,0:T(8,128)S(1)}, bf16[2,16,256,384]{3,2,1,0:T(8,128)(2,1)}) fusion(bf16[1,1536,384]{2,1,0:T(8,128)(2,1)S(1)} %copy-done.11, bf16[2,16,256,384]{3,2,1,0:T(8,128)(2,1)} %copy-done.1, bf16[2,16,256,1536]{3,2,1,0:T(8,128)(2,1)} %fusion.9.clone.3.clone.7), kind=kOutput, calls=%fused_computation.32.clone.2.clone | convolution fusion | flops 9679396864 | bytes 38961152 | tf_op jit(solution)/shard_map/while/body/eval_jaxpr/...f,fd->...d/dot_general | solution.py:64
  823.5 5.2 fusion.200
  835.2 95.8 %collective-permute-done.1 = f32[2,256,4]{1,2,0:T(4,128)S(1)} collective-permute-done((f32[2,256,4]{1,2,0:T(4,128)S(1)}, f32[2,256,4]{1,2,0:T(4,128)S(1)}, u32[]{:S(2)}, u32[]{:S(2)}) %collective-permute-start.1) | collective-permute-done | bytes 8224 | tf_op jit(solution)/shard_map/while/body/eval_jaxpr/ppermute | solution.py:97
  941.5 16.0 %convolution_convert_fusion.7 = bf16[2,16,256,3,6,64]{2,5,4,3,1,0:T(8,128)(2,1)} fusion(bf16[2,16,256,384]{3,2,1,0:T(8,128)(2,1)} %copy-done, f32[2,16,384]{2,1,0:T(8,128)S(1)} %get-tuple-element.467, f32[2,16,384]{2,1,0:T(8,128)S(1)} %get-tuple-element.468, f32[2,16,256]{2,1,0:T(8,128)S(1)} %add_rsqrt_fusion.12, ...), kind=kOutput, calls=%fused_computation.42.clone.1.clone | convolution fusion | flops 7276068864 | bytes 26214400 | tf_op jit(solution)/shard_map/while/body/eval_jaxpr/...d,dshe->...she/dot_general | solution.py:28
  957.5 25.2 %fusion.196 = (f32[2,16,6,256]{3,2,1,0:T(8,128)S(1)}, f32[2,16,6,256,256]{3,4,2,1,0:T(8,128)}) fusion(bf16[2,16,256,3,6,64]{2,5,4,3,1,0:T(8,128)(2,1)} %convolution_convert_fusion.7), kind=kOutput, calls=%fused_computation.163.clone.1.clone | convolution fusion | flops 1648361728 | bytes 63111168 | tf_op jit(solution)/shard_map/while/body/eval_jaxpr/sub | solution.py:34
  982.7 25.6 %convert_reduce_fusion.13 = (f32[2,16,256]{2,1,0:T(8,128)S(1)}, bf16[2,16,256,384]{3,2,1,0:T(8,128)(2,1)}) fusion(bf16[1,6,64,384]{3,2,1,0:T(8,128)(2,1)S(1)} %copy-done.14, f32[2,16,6,256,256]{3,4,2,1,0:T(8,128)} %get-tuple-element.470, f32[2,16,6,256]{3,2,1,0:T(8,128)S(1)} %get-tuple-element.471, ...), kind=kOutput, calls=%fused_computation.27.clone.1.clone | convolution fusion | flops 4070563840 | bytes 69730304 | tf_op jit(solution)/shard_map/while/body/eval_jaxpr/...qhe,hed->...qd/dot_general | solution.py:36
  1013.5 16.1 %convolution_convert_fusion.8 = bf16[2,16,256,3,6,64]{2,5,4,3,1,0:T(8,128)(2,1)} fusion(bf16[2,16,256,384]{3,2,1,0:T(8,128)(2,1)} %get-tuple-element.472, f32[2,16,384]{2,1,0:T(8,128)S(1)} %get-tuple-element.473, f32[2,16,384]{2,1,0:T(8,128)S(1)} %get-tuple-element.474, f32[2,16,256]{2,1,0:T(8,128)S(1)} %add_rsqrt_fusion.13, ...), kind=kOutput, calls=%fused_computation.41.clone.1.clone | convolution fusion | flops 7276068864 | bytes 26214400 | tf_op jit(solution)/shard_map/while/body/eval_jaxpr/...d,dshe->...she/dot_general | solution.py:28
  1029.6 8.1 slice.204
  1037.6 5.8 copy.94
  1043.5 9.4 collective-permute-start
  1052.9 7.8 slice_bitcast_fusion.56
  1060.7 18.5 %copy.96 = bf16[2,16,256,6,64]{4,1,3,2,0:T(8,128)(2,1)} copy(bf16[2,16,256,6,64]{2,4,3,1,0:T(8,128)(2,1)} %get-tuple-element.481) | data formatting | bytes 12582912 | tf_op jit(solution)/shard_map/while/body/eval_jaxpr/squeeze | solution.py:54
  1079.2 6.0 slice_bitcast_fusion.57
  1085.5 11.1 pad_maximum_fusion.10
  1096.6 35.4 %copy.97 = bf16[2,31,256,6,64]{4,1,3,2,0:T(8,128)(2,1)} copy(bf16[2,31,256,6,64]{2,4,3,1,0:T(8,128)(2,1)} %get-tuple-element.482) | data formatting | bytes 24379392 | tf_op jit(solution)/shard_map/while/body/eval_jaxpr/concatenate | solution.py:52
  1132.0 35.4 %copy.95 = bf16[2,31,256,6,64]{4,1,3,2,0:T(8,128)(2,1)} copy(bf16[2,31,256,6,64]{2,4,3,1,0:T(8,128)(2,1)} %get-tuple-element.480) | data formatting | bytes 24379392 | tf_op jit(solution)/shard_map/while/body/eval_jaxpr/concatenate | solution.py:53
  1167.4 28.3 %fusion.198 = (f32[2,256,6,16]{3,2,1,0:T(8,128)S(1)}, f32[2,256,6,16,31]{4,3,2,1,0:T(8,128)}) fusion(f32[6,16,31]{2,1,0:T(8,128)S(1)} %copy-done.2, bf16[2,16,256,6,64]{4,1,3,2,0:T(8,128)(2,1)} %copy.96, bf16[2,31,256,6,64]{4,1,3,2,0:T(8,128)(2,1)} %copy.97), kind=kOutput, calls=%fused_computation.164.clone.1.clone | convolution fusion | flops 201130016 | bytes 24784512 | tf_op jit(solution)/shard_map/while/body/eval_jaxpr/sub | solution.py:56
  1195.7 22.4 %convert_bitcast_fusion.3 = bf16[2,16,256,6,64]{4,1,3,2,0:T(8,128)(2,1)} fusion(bf16[2,31,256,6,64]{4,1,3,2,0:T(8,128)(2,1)} %copy.95, f32[2,256,6,16,31]{4,3,2,1,0:T(8,128)} %get-tuple-element.483, f32[2,256,6,16]{3,2,1,0:T(8,128)S(1)} %get-tuple-element.484), kind=kOutput, calls=%fused_computation.64.clone.1.clone | convolution fusion | flops 201228288 | bytes 24772608 | tf_op jit(solution)/shard_map/while/body/eval_jaxpr/...phfj,...jphe->...fphe/dot_general | solution.py:57
  1218.1 16.9 %convert_reduce_fusion.14 = (f32[2,16,256]{2,1,0:T(8,128)S(1)}, bf16[2,16,256,384]{3,2,1,0:T(8,128)(2,1)S(1)}) fusion(bf16[1,6,64,384]{3,2,1,0:T(8,128)(2,1)S(1)} %copy-done.15, bf16[2,16,256,6,64]{4,1,3,2,0:T(8,128)(2,1)} %convert_bitcast_fusion.3, bf16[2,16,256,384]{3,2,1,0:T(8,128)(2,1)} %get-tuple-element.472), kind=kOutput, calls=%fused_computation.24.clone.1.clone | convolution fusion | flops 2431639552 | bytes 19202048 | tf_op jit(solution)/shard_map/while/body/eval_jaxpr/...fphe,hed->...fpd/dot_general | solution.py:58
  1238.1 23.3 %fusion.9.clone.3.clone.7 = bf16[2,16,256,1536]{3,2,1,0:T(8,128)(2,1)} fusion(bf16[2,16,256,384]{3,2,1,0:T(8,128)(2,1)S(1)} %get-tuple-element.485, f32[2,16,384]{2,1,0:T(8,128)S(1)} %copy-done.8, f32[2,16,384]{2,1,0:T(8,128)S(1)} %copy-done.7, f32[2,16,256]{2,1,0:T(8,128)S(1)} %add_rsqrt_fusion.14, ...), kind=kOutput, calls=%fused_computation.11.clone.clone.clone.clone.clone.clone.clone.1.clone.1.clone | convolution fusion | flops 9795796992 | bytes 32800768 | tf_op jit(solution)/shard_map/while/body/eval_jaxpr/...d,df->...f/dot_general | solution.py:62
  1261.5 21.2 %convert_reduce_fusion.15 = (f32[2,16,256]{2,1,0:T(8,128)S(1)}, bf16[2,16,256,384]{3,2,1,0:T(8,128)(2,1)}) fusion(bf16[1,1536,384]{2,1,0:T(8,128)(2,1)S(1)} %copy-done.11, bf16[2,16,256,384]{3,2,1,0:T(8,128)(2,1)} %copy-done.1, bf16[2,16,256,1536]{3,2,1,0:T(8,128)(2,1)} %fusion.9.clone.3.clone.7), kind=kOutput, calls=%fused_computation.32.clone.2.clone | convolution fusion | flops 9679396864 | bytes 38961152 | tf_op jit(solution)/shard_map/while/body/eval_jaxpr/...f,fd->...d/dot_general | solution.py:64
  1282.7 5.2 fusion.200
  1294.4 95.9 %collective-permute-done.1 = f32[2,256,4]{1,2,0:T(4,128)S(1)} collective-permute-done((f32[2,256,4]{1,2,0:T(4,128)S(1)}, f32[2,256,4]{1,2,0:T(4,128)S(1)}, u32[]{:S(2)}, u32[]{:S(2)}) %collective-permute-start.1) | collective-permute-done | bytes 8224 | tf_op jit(solution)/shard_map/while/body/eval_jaxpr/ppermute | solution.py:97
  1396.0 60.9 %reduce-scatter.4.cloned.1.call-done = f32[16,24]{1,0:T(8,128)} async-done(((f32[256,24]{1,0:T(8,128)}), f32[16,24]{1,0:T(8,128)}) %reduce-scatter.4.cloned.1.call-update) | async-done | bytes 1552
  (238 shorter events, 78.1 us)
Async XLA Ops:
  7.2 1449.7 %reduce-scatter.4.cloned.1.call-start = ((), (), s32[]{:S(2)}) async-start(), calls=%async_computation.1 | async-start | bytes 139264
  14.9 25.4 %copy-start.3 = (f32[2,16,1,6,384]{4,1,0,3,2:T(8,128)}, f32[2,16,1,6,384]{4,1,0,3,2:T(8,128)S(1)}, u32[]{:S(2)}) copy-start(f32[2,16,1,6,384]{4,1,0,3,2:T(8,128)S(1)} %get-tuple-element.545) | copy-start | bytes 884740 | tf_op jit(solution)/shard_map/while
  14.9 25.4 %copy-start.5 = (f32[2,16,256,4]{2,3,1,0:T(4,128)}, f32[2,16,256,4]{2,3,1,0:T(4,128)S(1)}, u32[]{:S(2)}) copy-start(f32[2,16,256,4]{2,3,1,0:T(4,128)S(1)} %get-tuple-element.525) | copy-start | bytes 393220 | tf_op jit(solution)/shard_map/while
  40.3 25.2 %copy-start.14 = (bf16[1,6,64,384]{3,2,1,0:T(8,128)(2,1)S(1)}, bf16[1,6,64,384]{3,2,1,0:T(8,128)(2,1)}, u32[]{:S(2)}) copy-start(bf16[1,6,64,384]{3,2,1,0:T(8,128)(2,1)} %get-tuple-element.547) | copy-start | bytes 884740 | tf_op jit(solution)/shard_map/while
  65.6 30.7 %copy-start.13 = (bf16[1,384,3,6,64]{1,4,3,2,0:T(8,128)(2,1)S(1)}, bf16[1,384,3,6,64]{1,4,3,2,0:T(8,128)(2,1)}, u32[]{:S(2)}) copy-start(bf16[1,384,3,6,64]{1,4,3,2,0:T(8,128)(2,1)} %get-tuple-element.548) | copy-start | bytes 2654212 | tf_op jit(solution)/shard_map/while
  112.4 20.0 %slice-start = ((s8[18874368]{0:T(1024)(128)(4,1)}), s8[4194304]{0:T(1024)(128)(4,1)S(1)}, s32[]{:S(2)}) async-start(s8[18874368]{0:T(1024)(128)(4,1)} %bitcast.281), calls=%async_computation.2 | async-start | bytes 8388608 | tf_op jit(solution)/shard_map/while
  112.4 20.0 %slice-start.1 = ((s8[18874368]{0:T(1024)(128)(4,1)}), s8[4194304]{0:T(1024)(128)(4,1)S(1)}, s32[]{:S(2)}) async-start(s8[18874368]{0:T(1024)(128)(4,1)} %bitcast.281), calls=%async_computation.3 | async-start | bytes 8388608 | tf_op jit(solution)/shard_map/while
  112.4 20.0 %slice-start.2 = ((s8[18874368]{0:T(1024)(128)(4,1)}), s8[4194304]{0:T(1024)(128)(4,1)S(1)}, s32[]{:S(2)}) async-start(s8[18874368]{0:T(1024)(128)(4,1)} %bitcast.281), calls=%async_computation.4 | async-start | bytes 8388608 | tf_op jit(solution)/shard_map/while
  126.3 32.8 %collective-permute-start = (bf16[2,15,256,2,6,64]{2,5,4,1,0,3:T(8,128)(2,1)}, bf16[2,15,256,2,6,64]{2,5,4,1,0,3:T(8,128)(2,1)}, u32[]{:S(2)}, u32[]{:S(2)}) collective-permute-start(bf16[2,15,256,2,6,64]{2,5,4,1,0,3:T(8,128)(2,1)} %copy.94), channel_id=1, source_target_pairs={{0,1},{1,2},{2,3},{3,4},{4,5},{5,6},{6,7},{7,8},{8,9},{9,10},{10,1... | collective-permute-start | bytes 35389448 | tf_op jit(solution)/shard_map/while/body/eval_jaxpr/ppermute | solution.py:92
  211.9 35.4 %copy-start.2 = (f32[6,16,31]{2,1,0:T(8,128)S(1)}, f32[6,16,31]{2,1,0:T(8,128)}, u32[]{:S(2)}) copy-start(f32[6,16,31]{2,1,0:T(8,128)} %get-tuple-element.549) | copy-start | bytes 35716 | tf_op jit(solution)/shard_map/while
  275.6 22.4 %copy-start.15 = (bf16[1,6,64,384]{3,2,1,0:T(8,128)(2,1)S(1)}, bf16[1,6,64,384]{3,2,1,0:T(8,128)(2,1)}, u32[]{:S(2)}) copy-start(bf16[1,6,64,384]{3,2,1,0:T(8,128)(2,1)} %get-tuple-element.550) | copy-start | bytes 884740 | tf_op jit(solution)/shard_map/while
  298.0 20.0 %copy-start.7 = (f32[2,16,384]{2,1,0:T(8,128)S(1)}, f32[2,16,384]{2,1,0:T(8,128)}, u32[]{:S(2)}) copy-start(f32[2,16,384]{2,1,0:T(8,128)} %get-tuple-element.487) | copy-start | bytes 147460 | tf_op jit(solution)/shard_map/while
  298.0 20.0 %copy-start.8 = (f32[2,16,384]{2,1,0:T(8,128)S(1)}, f32[2,16,384]{2,1,0:T(8,128)}, u32[]{:S(2)}) copy-start(f32[2,16,384]{2,1,0:T(8,128)} %get-tuple-element.486) | copy-start | bytes 147460 | tf_op jit(solution)/shard_map/while
  298.0 20.0 %copy-start.10 = (bf16[1,384,1536]{2,1,0:T(8,128)(2,1)S(1)}, bf16[1,384,1536]{2,1,0:T(8,128)(2,1)}, u32[]{:S(2)}) copy-start(bf16[1,384,1536]{2,1,0:T(8,128)(2,1)} %get-tuple-element.551) | copy-start | bytes 3538948 | tf_op jit(solution)/shard_map/while
  314.8 26.4 %copy-start.1 = (bf16[2,16,256,384]{3,2,1,0:T(8,128)(2,1)}, bf16[2,16,256,384]{3,2,1,0:T(8,128)(2,1)S(1)}, u32[]{:S(2)}) copy-start(bf16[2,16,256,384]{3,2,1,0:T(8,128)(2,1)S(1)} %get-tuple-element.485) | copy-start | bytes 18874372 | tf_op jit(solution)/shard_map/while
  318.0 23.3 %copy-start.11 = (bf16[1,1536,384]{2,1,0:T(8,128)(2,1)S(1)}, bf16[1,1536,384]{2,1,0:T(8,128)(2,1)}, u32[]{:S(2)}) copy-start(bf16[1,1536,384]{2,1,0:T(8,128)(2,1)} %get-tuple-element.552) | copy-start | bytes 3538948 | tf_op jit(solution)/shard_map/while
  341.3 26.3 %copy-start.6 = (f32[2,16,256,4]{2,3,1,0:T(4,128)S(1)}, f32[2,16,256,4]{2,3,1,0:T(4,128)}, u32[]{:S(2)}) copy-start(f32[2,16,256,4]{2,3,1,0:T(4,128)} %copy-done.5) | copy-start | bytes 393220 | tf_op jit(solution)/shard_map/while
  341.3 26.3 %copy-start.9 = (f32[2,16,1,1]{1,0,3,2:T(2,128)S(1)}, f32[2,16,1,1]{1,0,3,2:T(2,128)}, u32[]{:S(2)}) copy-start(f32[2,16,1,1]{1,0,3,2:T(2,128)} %get-tuple-element.543) | copy-start | bytes 388 | tf_op jit(solution)/shard_map/while
  341.3 26.3 %copy-start.16 = (bf16[384,4]{0,1:T(4,128)(2,1)S(1)}, bf16[384,4]{0,1:T(4,128)(2,1)}, u32[]{:S(2)}) copy-start(bf16[384,4]{0,1:T(4,128)(2,1)} %get-tuple-element.553) | copy-start | bytes 9220 | tf_op jit(solution)/shard_map/while
  362.3 110.2 %copy-start.4 = (f32[2,16,1,6,384]{4,1,0,3,2:T(8,128)S(1)}, f32[2,16,1,6,384]{4,1,0,3,2:T(8,128)}, u32[]{:S(2)}) copy-start(f32[2,16,1,6,384]{4,1,0,3,2:T(8,128)} %copy-done.3) | copy-start | bytes 884740 | tf_op jit(solution)/shard_map/while
  372.1 99.7 %collective-permute-start.1 = (f32[2,256,4]{1,2,0:T(4,128)S(1)}, f32[2,256,4]{1,2,0:T(4,128)S(1)}, u32[]{:S(2)}, u32[]{:S(2)}) collective-permute-start(f32[2,256,4]{1,2,0:T(4,128)S(1)} %slice_bitcast_fusion.58), channel_id=1, source_target_pairs={{1,0},{2,1},{3,2},{4,3},{5,4},{6,5},{7,6},{8,7},{9,8},{10,9},{11,1... | collective-permute-start | bytes 24584 | tf_op jit(solution)/shard_map/while/body/eval_jaxpr/ppermute | solution.py:97
  473.0 25.5 %copy-start.3 = (f32[2,16,1,6,384]{4,1,0,3,2:T(8,128)}, f32[2,16,1,6,384]{4,1,0,3,2:T(8,128)S(1)}, u32[]{:S(2)}) copy-start(f32[2,16,1,6,384]{4,1,0,3,2:T(8,128)S(1)} %get-tuple-element.545) | copy-start | bytes 884740 | tf_op jit(solution)/shard_map/while
  473.0 25.5 %copy-start.5 = (f32[2,16,256,4]{2,3,1,0:T(4,128)}, f32[2,16,256,4]{2,3,1,0:T(4,128)S(1)}, u32[]{:S(2)}) copy-start(f32[2,16,256,4]{2,3,1,0:T(4,128)S(1)} %get-tuple-element.525) | copy-start | bytes 393220 | tf_op jit(solution)/shard_map/while
  498.4 25.2 %copy-start.14 = (bf16[1,6,64,384]{3,2,1,0:T(8,128)(2,1)S(1)}, bf16[1,6,64,384]{3,2,1,0:T(8,128)(2,1)}, u32[]{:S(2)}) copy-start(bf16[1,6,64,384]{3,2,1,0:T(8,128)(2,1)} %get-tuple-element.547) | copy-start | bytes 884740 | tf_op jit(solution)/shard_map/while
  523.7 30.6 %copy-start.13 = (bf16[1,384,3,6,64]{1,4,3,2,0:T(8,128)(2,1)S(1)}, bf16[1,384,3,6,64]{1,4,3,2,0:T(8,128)(2,1)}, u32[]{:S(2)}) copy-start(bf16[1,384,3,6,64]{1,4,3,2,0:T(8,128)(2,1)} %get-tuple-element.548) | copy-start | bytes 2654212 | tf_op jit(solution)/shard_map/while
  570.4 23.4 %slice-start = ((s8[18874368]{0:T(1024)(128)(4,1)}), s8[4194304]{0:T(1024)(128)(4,1)S(1)}, s32[]{:S(2)}) async-start(s8[18874368]{0:T(1024)(128)(4,1)} %bitcast.281), calls=%async_computation.2 | async-start | bytes 8388608 | tf_op jit(solution)/shard_map/while
  570.4 23.4 %slice-start.1 = ((s8[18874368]{0:T(1024)(128)(4,1)}), s8[4194304]{0:T(1024)(128)(4,1)S(1)}, s32[]{:S(2)}) async-start(s8[18874368]{0:T(1024)(128)(4,1)} %bitcast.281), calls=%async_computation.3 | async-start | bytes 8388608 | tf_op jit(solution)/shard_map/while
  570.4 23.4 %slice-start.2 = ((s8[18874368]{0:T(1024)(128)(4,1)}), s8[4194304]{0:T(1024)(128)(4,1)S(1)}, s32[]{:S(2)}) async-start(s8[18874368]{0:T(1024)(128)(4,1)} %bitcast.281), calls=%async_computation.4 | async-start | bytes 8388608 | tf_op jit(solution)/shard_map/while
  578.4 15.3 %slice-start.3 = ((s8[18874368]{0:T(1024)(128)(4,1)}), s8[4194304]{0:T(1024)(128)(4,1)S(1)}, s32[]{:S(2)}) async-start(s8[18874368]{0:T(1024)(128)(4,1)} %bitcast.281), calls=%async_computation.5 | async-start | bytes 8388608 | tf_op jit(solution)/shard_map/while
  578.5 15.3 %slice-start.4 = ((s8[18874368]{0:T(1024)(128)(4,1)}), s8[2097152]{0:T(1024)(128)(4,1)S(1)}, s32[]{:S(2)}) async-start(s8[18874368]{0:T(1024)(128)(4,1)} %bitcast.281), calls=%async_computation.6 | async-start | bytes 4194304 | tf_op jit(solution)/shard_map/while
  584.3 35.8 %collective-permute-start = (bf16[2,15,256,2,6,64]{2,5,4,1,0,3:T(8,128)(2,1)}, bf16[2,15,256,2,6,64]{2,5,4,1,0,3:T(8,128)(2,1)}, u32[]{:S(2)}, u32[]{:S(2)}) collective-permute-start(bf16[2,15,256,2,6,64]{2,5,4,1,0,3:T(8,128)(2,1)} %copy.94), channel_id=1, source_target_pairs={{0,1},{1,2},{2,3},{3,4},{4,5},{5,6},{6,7},{7,8},{8,9},{9,10},{10,1... | collective-permute-start | bytes 35389448 | tf_op jit(solution)/shard_map/while/body/eval_jaxpr/ppermute | solution.py:92
  672.9 35.4 %copy-start.2 = (f32[6,16,31]{2,1,0:T(8,128)S(1)}, f32[6,16,31]{2,1,0:T(8,128)}, u32[]{:S(2)}) copy-start(f32[6,16,31]{2,1,0:T(8,128)} %get-tuple-element.549) | copy-start | bytes 35716 | tf_op jit(solution)/shard_map/while
  736.6 22.4 %copy-start.15 = (bf16[1,6,64,384]{3,2,1,0:T(8,128)(2,1)S(1)}, bf16[1,6,64,384]{3,2,1,0:T(8,128)(2,1)}, u32[]{:S(2)}) copy-start(bf16[1,6,64,384]{3,2,1,0:T(8,128)(2,1)} %get-tuple-element.550) | copy-start | bytes 884740 | tf_op jit(solution)/shard_map/while
  758.9 20.1 %copy-start.7 = (f32[2,16,384]{2,1,0:T(8,128)S(1)}, f32[2,16,384]{2,1,0:T(8,128)}, u32[]{:S(2)}) copy-start(f32[2,16,384]{2,1,0:T(8,128)} %get-tuple-element.487) | copy-start | bytes 147460 | tf_op jit(solution)/shard_map/while
  758.9 20.1 %copy-start.8 = (f32[2,16,384]{2,1,0:T(8,128)S(1)}, f32[2,16,384]{2,1,0:T(8,128)}, u32[]{:S(2)}) copy-start(f32[2,16,384]{2,1,0:T(8,128)} %get-tuple-element.486) | copy-start | bytes 147460 | tf_op jit(solution)/shard_map/while
  759.0 20.1 %copy-start.10 = (bf16[1,384,1536]{2,1,0:T(8,128)(2,1)S(1)}, bf16[1,384,1536]{2,1,0:T(8,128)(2,1)}, u32[]{:S(2)}) copy-start(bf16[1,384,1536]{2,1,0:T(8,128)(2,1)} %get-tuple-element.551) | copy-start | bytes 3538948 | tf_op jit(solution)/shard_map/while
  776.0 26.5 %copy-start.1 = (bf16[2,16,256,384]{3,2,1,0:T(8,128)(2,1)}, bf16[2,16,256,384]{3,2,1,0:T(8,128)(2,1)S(1)}, u32[]{:S(2)}) copy-start(bf16[2,16,256,384]{3,2,1,0:T(8,128)(2,1)S(1)} %get-tuple-element.485) | copy-start | bytes 18874372 | tf_op jit(solution)/shard_map/while
  779.1 23.4 %copy-start.11 = (bf16[1,1536,384]{2,1,0:T(8,128)(2,1)S(1)}, bf16[1,1536,384]{2,1,0:T(8,128)(2,1)}, u32[]{:S(2)}) copy-start(bf16[1,1536,384]{2,1,0:T(8,128)(2,1)} %get-tuple-element.552) | copy-start | bytes 3538948 | tf_op jit(solution)/shard_map/while
  802.5 26.3 %copy-start.6 = (f32[2,16,256,4]{2,3,1,0:T(4,128)S(1)}, f32[2,16,256,4]{2,3,1,0:T(4,128)}, u32[]{:S(2)}) copy-start(f32[2,16,256,4]{2,3,1,0:T(4,128)} %copy-done.5) | copy-start | bytes 393220 | tf_op jit(solution)/shard_map/while
  802.5 26.3 %copy-start.9 = (f32[2,16,1,1]{1,0,3,2:T(2,128)S(1)}, f32[2,16,1,1]{1,0,3,2:T(2,128)}, u32[]{:S(2)}) copy-start(f32[2,16,1,1]{1,0,3,2:T(2,128)} %get-tuple-element.543) | copy-start | bytes 388 | tf_op jit(solution)/shard_map/while
  802.5 26.3 %copy-start.16 = (bf16[384,4]{0,1:T(4,128)(2,1)S(1)}, bf16[384,4]{0,1:T(4,128)(2,1)}, u32[]{:S(2)}) copy-start(bf16[384,4]{0,1:T(4,128)(2,1)} %get-tuple-element.553) | copy-start | bytes 9220 | tf_op jit(solution)/shard_map/while
  823.5 108.2 %copy-start.4 = (f32[2,16,1,6,384]{4,1,0,3,2:T(8,128)S(1)}, f32[2,16,1,6,384]{4,1,0,3,2:T(8,128)}, u32[]{:S(2)}) copy-start(f32[2,16,1,6,384]{4,1,0,3,2:T(8,128)} %copy-done.3) | copy-start | bytes 884740 | tf_op jit(solution)/shard_map/while
  833.3 97.7 %collective-permute-start.1 = (f32[2,256,4]{1,2,0:T(4,128)S(1)}, f32[2,256,4]{1,2,0:T(4,128)S(1)}, u32[]{:S(2)}, u32[]{:S(2)}) collective-permute-start(f32[2,256,4]{1,2,0:T(4,128)S(1)} %slice_bitcast_fusion.58), channel_id=1, source_target_pairs={{1,0},{2,1},{3,2},{4,3},{5,4},{6,5},{7,6},{8,7},{9,8},{10,9},{11,1... | collective-permute-start | bytes 24584 | tf_op jit(solution)/shard_map/while/body/eval_jaxpr/ppermute | solution.py:97
  932.0 25.5 %copy-start.3 = (f32[2,16,1,6,384]{4,1,0,3,2:T(8,128)}, f32[2,16,1,6,384]{4,1,0,3,2:T(8,128)S(1)}, u32[]{:S(2)}) copy-start(f32[2,16,1,6,384]{4,1,0,3,2:T(8,128)S(1)} %get-tuple-element.545) | copy-start | bytes 884740 | tf_op jit(solution)/shard_map/while
  932.0 25.5 %copy-start.5 = (f32[2,16,256,4]{2,3,1,0:T(4,128)}, f32[2,16,256,4]{2,3,1,0:T(4,128)S(1)}, u32[]{:S(2)}) copy-start(f32[2,16,256,4]{2,3,1,0:T(4,128)S(1)} %get-tuple-element.525) | copy-start | bytes 393220 | tf_op jit(solution)/shard_map/while
  957.5 25.2 %copy-start.14 = (bf16[1,6,64,384]{3,2,1,0:T(8,128)(2,1)S(1)}, bf16[1,6,64,384]{3,2,1,0:T(8,128)(2,1)}, u32[]{:S(2)}) copy-start(bf16[1,6,64,384]{3,2,1,0:T(8,128)(2,1)} %get-tuple-element.547) | copy-start | bytes 884740 | tf_op jit(solution)/shard_map/while
  982.7 30.8 %copy-start.13 = (bf16[1,384,3,6,64]{1,4,3,2,0:T(8,128)(2,1)S(1)}, bf16[1,384,3,6,64]{1,4,3,2,0:T(8,128)(2,1)}, u32[]{:S(2)}) copy-start(bf16[1,384,3,6,64]{1,4,3,2,0:T(8,128)(2,1)} %get-tuple-element.548) | copy-start | bytes 2654212 | tf_op jit(solution)/shard_map/while
  1029.5 23.3 %slice-start = ((s8[18874368]{0:T(1024)(128)(4,1)}), s8[4194304]{0:T(1024)(128)(4,1)S(1)}, s32[]{:S(2)}) async-start(s8[18874368]{0:T(1024)(128)(4,1)} %bitcast.281), calls=%async_computation.2 | async-start | bytes 8388608 | tf_op jit(solution)/shard_map/while
  1029.5 23.3 %slice-start.1 = ((s8[18874368]{0:T(1024)(128)(4,1)}), s8[4194304]{0:T(1024)(128)(4,1)S(1)}, s32[]{:S(2)}) async-start(s8[18874368]{0:T(1024)(128)(4,1)} %bitcast.281), calls=%async_computation.3 | async-start | bytes 8388608 | tf_op jit(solution)/shard_map/while
  1029.5 23.3 %slice-start.2 = ((s8[18874368]{0:T(1024)(128)(4,1)}), s8[4194304]{0:T(1024)(128)(4,1)S(1)}, s32[]{:S(2)}) async-start(s8[18874368]{0:T(1024)(128)(4,1)} %bitcast.281), calls=%async_computation.4 | async-start | bytes 8388608 | tf_op jit(solution)/shard_map/while
  1037.6 15.3 %slice-start.3 = ((s8[18874368]{0:T(1024)(128)(4,1)}), s8[4194304]{0:T(1024)(128)(4,1)S(1)}, s32[]{:S(2)}) async-start(s8[18874368]{0:T(1024)(128)(4,1)} %bitcast.281), calls=%async_computation.5 | async-start | bytes 8388608 | tf_op jit(solution)/shard_map/while
  1043.5 35.7 %collective-permute-start = (bf16[2,15,256,2,6,64]{2,5,4,1,0,3:T(8,128)(2,1)}, bf16[2,15,256,2,6,64]{2,5,4,1,0,3:T(8,128)(2,1)}, u32[]{:S(2)}, u32[]{:S(2)}) collective-permute-start(bf16[2,15,256,2,6,64]{2,5,4,1,0,3:T(8,128)(2,1)} %copy.94), channel_id=1, source_target_pairs={{0,1},{1,2},{2,3},{3,4},{4,5},{5,6},{6,7},{7,8},{8,9},{9,10},{10,1... | collective-permute-start | bytes 35389448 | tf_op jit(solution)/shard_map/while/body/eval_jaxpr/ppermute | solution.py:92
  1132.0 35.4 %copy-start.2 = (f32[6,16,31]{2,1,0:T(8,128)S(1)}, f32[6,16,31]{2,1,0:T(8,128)}, u32[]{:S(2)}) copy-start(f32[6,16,31]{2,1,0:T(8,128)} %get-tuple-element.549) | copy-start | bytes 35716 | tf_op jit(solution)/shard_map/while
  1195.6 22.4 %copy-start.15 = (bf16[1,6,64,384]{3,2,1,0:T(8,128)(2,1)S(1)}, bf16[1,6,64,384]{3,2,1,0:T(8,128)(2,1)}, u32[]{:S(2)}) copy-start(bf16[1,6,64,384]{3,2,1,0:T(8,128)(2,1)} %get-tuple-element.550) | copy-start | bytes 884740 | tf_op jit(solution)/shard_map/while
  1218.0 20.1 %copy-start.7 = (f32[2,16,384]{2,1,0:T(8,128)S(1)}, f32[2,16,384]{2,1,0:T(8,128)}, u32[]{:S(2)}) copy-start(f32[2,16,384]{2,1,0:T(8,128)} %get-tuple-element.487) | copy-start | bytes 147460 | tf_op jit(solution)/shard_map/while
  1218.0 20.1 %copy-start.8 = (f32[2,16,384]{2,1,0:T(8,128)S(1)}, f32[2,16,384]{2,1,0:T(8,128)}, u32[]{:S(2)}) copy-start(f32[2,16,384]{2,1,0:T(8,128)} %get-tuple-element.486) | copy-start | bytes 147460 | tf_op jit(solution)/shard_map/while
  1218.0 20.1 %copy-start.10 = (bf16[1,384,1536]{2,1,0:T(8,128)(2,1)S(1)}, bf16[1,384,1536]{2,1,0:T(8,128)(2,1)}, u32[]{:S(2)}) copy-start(bf16[1,384,1536]{2,1,0:T(8,128)(2,1)} %get-tuple-element.551) | copy-start | bytes 3538948 | tf_op jit(solution)/shard_map/while
  1235.0 26.5 %copy-start.1 = (bf16[2,16,256,384]{3,2,1,0:T(8,128)(2,1)}, bf16[2,16,256,384]{3,2,1,0:T(8,128)(2,1)S(1)}, u32[]{:S(2)}) copy-start(bf16[2,16,256,384]{3,2,1,0:T(8,128)(2,1)S(1)} %get-tuple-element.485) | copy-start | bytes 18874372 | tf_op jit(solution)/shard_map/while
  1238.1 23.3 %copy-start.11 = (bf16[1,1536,384]{2,1,0:T(8,128)(2,1)S(1)}, bf16[1,1536,384]{2,1,0:T(8,128)(2,1)}, u32[]{:S(2)}) copy-start(bf16[1,1536,384]{2,1,0:T(8,128)(2,1)} %get-tuple-element.552) | copy-start | bytes 3538948 | tf_op jit(solution)/shard_map/while
  1261.4 26.5 %copy-start.6 = (f32[2,16,256,4]{2,3,1,0:T(4,128)S(1)}, f32[2,16,256,4]{2,3,1,0:T(4,128)}, u32[]{:S(2)}) copy-start(f32[2,16,256,4]{2,3,1,0:T(4,128)} %copy-done.5) | copy-start | bytes 393220 | tf_op jit(solution)/shard_map/while
  1261.4 26.5 %copy-start.9 = (f32[2,16,1,1]{1,0,3,2:T(2,128)S(1)}, f32[2,16,1,1]{1,0,3,2:T(2,128)}, u32[]{:S(2)}) copy-start(f32[2,16,1,1]{1,0,3,2:T(2,128)} %get-tuple-element.543) | copy-start | bytes 388 | tf_op jit(solution)/shard_map/while
  1261.5 26.5 %copy-start.16 = (bf16[384,4]{0,1:T(4,128)(2,1)S(1)}, bf16[384,4]{0,1:T(4,128)(2,1)}, u32[]{:S(2)}) copy-start(bf16[384,4]{0,1:T(4,128)(2,1)} %get-tuple-element.553) | copy-start | bytes 9220 | tf_op jit(solution)/shard_map/while
  1282.7 108.3 %copy-start.4 = (f32[2,16,1,6,384]{4,1,0,3,2:T(8,128)S(1)}, f32[2,16,1,6,384]{4,1,0,3,2:T(8,128)}, u32[]{:S(2)}) copy-start(f32[2,16,1,6,384]{4,1,0,3,2:T(8,128)} %copy-done.3) | copy-start | bytes 884740 | tf_op jit(solution)/shard_map/while
  1292.5 97.8 %collective-permute-start.1 = (f32[2,256,4]{1,2,0:T(4,128)S(1)}, f32[2,256,4]{1,2,0:T(4,128)S(1)}, u32[]{:S(2)}, u32[]{:S(2)}) collective-permute-start(f32[2,256,4]{1,2,0:T(4,128)S(1)} %slice_bitcast_fusion.58), channel_id=1, source_target_pairs={{1,0},{2,1},{3,2},{4,3},{5,4},{6,5},{7,6},{8,7},{9,8},{10,9},{11,1... | collective-permute-start | bytes 24584 | tf_op jit(solution)/shard_map/while/body/eval_jaxpr/ppermute | solution.py:97
  (15 other events, 112.4 us)
Sparse Core Ops, SparseCore 0:
  1395.5 61.3 reduce-scatter.3
where the time goes:
time: 1480 us; the launch traced here: 1470 us
  matrix products  607 us (41%)
  local copies, waits for them, and re-layouts  370 us (25%)
  waiting for transfers between devices  350 us (24%)
  other arithmetic  92.1 us (6%)
  starting transfers between devices  28.9 us (2%)
    ppermute x3, waiting for transfers between devices, step(): from_next = lax.ppermute(updated[:, 0], 'frames', to_prev)  289 us
    concatenate x3, local copies, waits for them, and re-layouts, temporal_mix(): jnp.concatenate([halo[..., 1, :, :], projected[..., 2, :, :]], axis=-4)  106 us
    concatenate x3, local copies, waits for them, and re-layouts, temporal_mix(): jnp.concatenate([halo[..., 0, :, :], projected[..., 1, :, :]], axis=-4)  106 us
    dot_general x6, matrix products, project_qkv(): jnp.einsum('...d,dshe->...she', normed, w_qkv, preferred_element_type=jnp...  96.2 us
    sub x3, matrix products, temporal_mix(): attn_probs = jax.nn.softmax(scores, axis=-1).astype(jnp.bfloat16)  84.8 us
    dot_general x3, matrix products, spatial_mix(): jnp.einsum('...qhe,hed->...qd', mixed, w_proj, preferred_element_type=jnp...  76.6 us
    sub x3, matrix products, spatial_mix(): attn_probs = jax.nn.softmax(scores, axis=-1).astype(jnp.bfloat16)  75.6 us
    dot_general x3, matrix products, mlp_mix(): jnp.einsum('...d,df->...f', normed, w_up, preferred_element_type=jnp.floa...  69.9 us
  transfers between devices with their start and end apart: 7, of which 4 were waited for; matrix products, arithmetic and copies ran while one was open for 6% of the time, Pallas kernels for 0%

commit v1 on v0

v1 whole, which is shorter than its diff:
```python
import functools
import jax
import jax.numpy as jnp
from jax import lax
from jax.experimental import pallas as pl
from jax.experimental.pallas import tpu as pltpu
from jax.sharding import PartitionSpec as P

LN_EPS = 1e-6
MASKED = -1e30
LOG2E = 1.4426950408889634
F32 = jnp.float32
BF16 = jnp.bfloat16


def mm(lhs, rhs, lc, rc):
    return lax.dot_general(lhs, rhs, (((lc,), (rc,)), ((), ())), preferred_element_type=F32)


def norm_rows(x):
    centered = x - jnp.mean(x, axis=-1, keepdims=True)
    return centered * lax.rsqrt(jnp.mean(centered * centered, axis=-1, keepdims=True) + LN_EPS)


def norm_cols(x):
    centered = x - jnp.mean(x, axis=0, keepdims=True)
    return centered * lax.rsqrt(jnp.mean(centered * centered, axis=0, keepdims=True) + LN_EPS)


def pipelined(items, scores, weigh, mix, ahead=2, behind=2):
    raw, weighed = {}, {}
    count = len(items)
    for n in range(-ahead, count + behind):
        if n + ahead < count:
            raw[n + ahead] = scores(items[n + ahead])
        if 0 <= n < count:
            weighed[n] = weigh(items[n], raw.pop(n))
        if 0 <= n - behind < count:
            mix(items[n - behind], weighed.pop(n - behind))


def spatial(u, wqkv_t, wo, heads):
    rows, dim = u.shape
    half = rows // 2
    width = dim // heads
    qkv = mm(wqkv_t, u, 1, 1).astype(BF16)
    outs = {}

    def part(index, h, f):
        return qkv[index * dim + h * width:index * dim + (h + 1) * width, f * half:(f + 1) * half]

    items = [(h, f) for h in range(heads) for f in range(2)]
    keys = {item: part(1, *item).T for item in items}

    def scores(item):
        return mm(keys[item], part(0, *item), 1, 0)

    def weigh(item, s):
        p = jnp.exp2((s - jnp.max(s, axis=0, keepdims=True)) * (LOG2E * width ** -0.5))
        return p.astype(BF16), 1.0 / jnp.sum(p, axis=0, keepdims=True)

    def mix(item, weighed):
        outs[item] = (mm(part(2, *item), weighed[0], 1, 0) * weighed[1]).astype(BF16)

    pipelined(items, scores, weigh, mix)
    mixed = jnp.concatenate([jnp.concatenate([outs[h, f] for f in range(2)], axis=1) for h in range(heads)], axis=0)
    return mm(mixed, wo, 0, 0)


def pair_rows(first, second):
    rows, dim = first.shape
    both = jnp.concatenate([first.reshape(rows // 8, 1, 8, dim), second.reshape(rows // 8, 1, 8, dim)], axis=1)
    return both.reshape(2 * rows, dim)


def pair_mod(x, scale, shift):
    rows, dim = x.shape
    x = x.reshape(rows // 16, 2, 8, dim)
    return (x * scale[None, :, None, :] + shift[None, :, None, :]).reshape(rows, dim)


def stage_a(heads, z_ref, mod_ref, w_in, wqkv_t, wo, x_ref, u_ref):
    tokens = z_ref.shape[1]
    z = jnp.concatenate([z_ref[0], z_ref[1]], axis=0).astype(BF16)
    x0 = mm(z, w_in[...], 1, 0).astype(BF16).astype(F32)
    n0 = norm_rows(x0)
    u = jnp.concatenate([n0[s * tokens:(s + 1) * tokens] * (1.0 + mod_ref[s, 1:2]) + mod_ref[s, 0:1] for s in range(2)], axis=0).astype(BF16)
    x = x0 + spatial(u, wqkv_t[...], wo[...], heads)
    x = pair_rows(x[:tokens], x[tokens:]).astype(BF16)
    x_ref[0] = x
    u_ref[0] = pair_mod(norm_rows(x.astype(F32)), 1.0 + mod_ref[:, 3], mod_ref[:, 2]).astype(BF16)


def stage_t(heads, halo_ref, own_ref, wqkv_t, bias_ref, o_ref):
    dim = own_ref.shape[-1]
    width = dim // heads
    groups = own_ref.shape[1] // 16
    own = [own_ref[:, g * 16:(g + 1) * 16].reshape(-1, dim) for g in range(groups)]
    halo = [halo_ref[:, g * 16:(g + 1) * 16].reshape(-1, dim) for g in range(groups)]
    queries = own[0].shape[0]
    keys = 2 * queries
    q_all = (mm(wqkv_t[:dim], jnp.concatenate(own, axis=0), 1, 1) * width ** -0.5).astype(BF16)
    kv_all = mm(wqkv_t[dim:], jnp.concatenate([b for g in range(groups) for b in (halo[g], own[g])], axis=0), 1, 1).astype(BF16)
    sub = lax.broadcasted_iota(jnp.int32, (keys, 2 * queries), 0) % 8
    lane = lax.broadcasted_iota(jnp.int32, (keys, 2 * queries), 1) % 8
    same = sub == lane
    outs = {}
    items = [(pair, g) for pair in range(heads // 2) for g in range(groups)]
    rows = lambda pair: slice(2 * pair * width, 2 * (pair + 1) * width)
    k_rows = {(pair, g): kv_all[rows(pair), g * keys:(g + 1) * keys].T for pair, g in items}
    zero = jnp.zeros((width, queries), BF16)

    def scores(item):
        pair, g = item
        q = q_all[rows(pair), g * queries:(g + 1) * queries]
        q = jnp.concatenate([jnp.concatenate([q[:width], zero], axis=1), jnp.concatenate([zero, q[width:]], axis=1)], axis=0)
        return mm(k_rows[item], q, 1, 0)

    def weigh(item, s):
        pair, g = item
        s = s.reshape(keys // 8, 8, 2 * queries) + bias_ref[:, :, 2 * pair * queries:2 * (pair + 1) * queries]
        p = jnp.exp2((s - jnp.max(s, axis=0, keepdims=True)) * LOG2E)
        total = jnp.sum(p, axis=0)
        total = jnp.sum(jnp.where(same[:8], total, 0.0), axis=0, keepdims=True)
        return jnp.where(same, p.reshape(keys, 2 * queries), 0.0).astype(BF16), 1.0 / total

    def mix(item, weighed):
        pair, g = item
        mixed = mm(kv_all[dim + 2 * pair * width:dim + 2 * (pair + 1) * width, g * keys:(g + 1) * keys], weighed[0], 1, 0) * weighed[1]
        outs[item] = jnp.concatenate([mixed[:width, :queries], mixed[width:, queries:]], axis=0).astype(BF16)

    pipelined(items, scores, weigh, mix)
    for g in range(groups):
        o = jnp.concatenate([outs[pair, g] for pair in range(heads // 2)], axis=0)
        o_ref[:, g * 16:(g + 1) * 16] = o.T.reshape(-1, 16, dim)


def stage_m(o_ref, x_ref, mod_ref, dt_ref, z_ref, wo, w_up_t, w_down_t, w_out_t, out_ref):
    x = (x_ref[0].astype(F32) + mm(o_ref[0], wo[...], 1, 0)).astype(BF16)
    u = pair_mod(norm_rows(x.astype(F32)), 0.5 * (1.0 + mod_ref[:, 5]), 0.5 * mod_ref[:, 4]).astype(BF16)
    first = 2 * pl.program_id(0)
    tokens = x.shape[0] // 2
    h = mm(w_up_t[...], u, 1, 1)
    t = jnp.tanh(h * (1.5957691216057308 + 0.285419265090401 * (h * h)))
    h = (h + h * t).astype(BF16)
    x_t = (x.T.astype(F32) + mm(w_down_t[...], h, 1, 0)).astype(BF16).astype(F32)
    v = mm(w_out_t[...], norm_cols(x_t).astype(BF16), 1, 0)[:8].T
    v = v.reshape(tokens // 8, 2, 8, 8)
    for s in range(2):
        out_ref[s] = z_ref[s] + dt_ref[first + s] * v[:, s].reshape(tokens, 8)[:, :4]


def solution(mesh):
    group = mesh.shape['frames']
    slot_spec = P(('videos', 'frames'))
    emit_spec = P('videos', 'frames')
    whole = P()
    to_next = [(source, source + 1) for source in range(group - 1)]
    to_prev = [(source + 1, source) for source in range(group - 1)]

    def local(latents_a, mod_a, dt_a, noise_a, latents_b, mod_b, dt_b, noise_b, w_in, sp_qkv, sp_out, tm_qkv, tm_bias, tm_out, mlp_up, mlp_down, w_out):
        position = lax.axis_index('frames')
        slots, tokens, channels = latents_a.shape
        dim = w_in.shape[1]
        heads = tm_bias.shape[1]
        window = tm_bias.shape[-1]
        pairs = slots // 2
        full = lambda a: pl.BlockSpec(a.shape, lambda i: (0,) * a.ndim, pipeline_mode=pl.Buffered(1))
        sp_t = jnp.transpose(sp_qkv[0], (1, 2, 3, 0)).reshape(3 * dim, dim)
        tm_t = jnp.transpose(tm_qkv[0], (1, 2, 3, 0)).reshape(3 * dim, dim)
        sp_o = sp_out[0].reshape(dim, dim)
        tm_o = tm_out[0].reshape(dim, dim)
        up_t = mlp_up[0].T
        down_t = mlp_down[0].T
        out_t = jnp.pad(w_out.T, ((0, 16 - channels), (0, 0)))
        offset = jnp.arange(slots)[None, :] + slots - jnp.arange(2 * slots)[:, None]
        keep = (offset >= 0) & (offset < window) & ((jnp.arange(2 * slots)[:, None] >= slots) | (position > 0))
        table = jnp.where(keep[:, None], jnp.take(tm_bias[0], jnp.clip(offset, 0, window - 1), axis=1).transpose(1, 0, 2), MASKED)
        table = jnp.broadcast_to(table[:, None, :, :, None], (2 * slots, 8, heads, slots, 8)).reshape(2 * slots, 8, heads * slots * 8)
        params = pltpu.CompilerParams(vmem_limit_bytes=60 * 1024 * 1024)
        pair_block = lambda: pl.BlockSpec((1, 2 * tokens, dim), lambda i: (i, 0, 0))
        slot_block = lambda *rest: pl.BlockSpec((2, *rest), lambda i: (i,) + (0,) * len(rest))
        act = jax.ShapeDtypeStruct((pairs, 2 * tokens, dim), BF16)

        def call_a(z, mod):
            return pl.pallas_call(
                functools.partial(stage_a, heads), grid=(pairs,),
                in_specs=[slot_block(tokens, channels), slot_block(6, dim), full(w_in), full(sp_t), full(sp_o)],
                out_specs=[pair_block(), pair_block()], out_shape=[act, act], compiler_params=params, name='stage_a',
                cost_estimate=pl.CostEstimate(flops=20 * 10**9, bytes_accessed=12 * 10**6, transcendentals=0),
            )(z, mod, w_in, sp_t, sp_o)

        def call_t(halo, own):
            block = lambda: pl.BlockSpec((pairs, 32, dim), lambda i: (0, i, 0))
            return pl.pallas_call(
                functools.partial(stage_t, heads), grid=(tokens // 16,),
                in_specs=[block(), block(), full(tm_t), full(table)],
                out_specs=block(), out_shape=act, compiler_params=params, name='stage_t',
                cost_estimate=pl.CostEstimate(flops=20 * 10**9, bytes_accessed=12 * 10**6, transcendentals=0),
            )(halo, own, tm_t, table)

        def call_m(o, x, mod, dt, z):
            return pl.pallas_call(
                stage_m, grid=(pairs,),
                in_specs=[pair_block(), pair_block(), slot_block(6, dim), pl.BlockSpec(memory_space=pltpu.SMEM), slot_block(tokens, channels),
                          full(tm_o), full(up_t), full(down_t), full(out_t)],
                out_specs=slot_block(tokens, channels), out_shape=jax.ShapeDtypeStruct((slots, tokens, channels), F32), compiler_params=params, name='stage_m',
                cost_estimate=pl.CostEstimate(flops=20 * 10**9, bytes_accessed=12 * 10**6, transcendentals=0),
            )(o, x, mod, dt, z, tm_o, up_t, down_t, out_t)

        mods = [mod_a[:, 0], mod_b[:, 0]]
        dts = [dt_a, dt_b]

        def step(queues, noise):
            front = [call_a(queues[n], mods[n]) for n in range(2)]
            halos = [lax.ppermute(front[n][1], 'frames', to_next) for n in range(2)]
            new, emitted = [], []
            for n in range(2):
                mixed = call_t(halos[n], front[n][1])
                updated = call_m(mixed, front[n][0], mods[n], dts[n], queues[n])
                from_next = lax.ppermute(updated[0], 'frames', to_prev)
                incoming = jnp.where(position == group - 1, noise[n], from_next)
                new.append(jnp.concatenate([updated[1:], incoming[None]], axis=0))
                emitted.append(updated[0])
            return tuple(new), jnp.stack(emitted)

        queues, emit = lax.scan(step, (latents_a, latents_b), (noise_a, noise_b))
        emit = jnp.moveaxis(emit, 1, 0).reshape(-1, tokens, channels)
        emit = lax.psum_scatter(jnp.where(position == 0, emit, 0.0), 'frames', scatter_dimension=1, tiled=True)
        half = emit.shape[0] // 2
        return emit[:half], queues[0], emit[half:], queues[1]

    return jax.shard_map(local, mesh=mesh, in_specs=(slot_spec, slot_spec, slot_spec, P('videos'), slot_spec, slot_spec, slot_spec, P('videos')) + (whole,) * 9, out_specs=(emit_spec, slot_spec, emit_spec, slot_spec), check_vma=False)
```

time: 1480 us -> 643 us (0.43)
  matrix products: 607 us -> 0 us
  Pallas kernels: 0 us -> 468 us
  local copies, waits for them, and re-layouts: 370 us -> 52.4 us
  waiting for transfers between devices: 350 us -> 68.8 us
  other arithmetic: 92.1 us -> 0.56 us
    pallas_call x0 -> x18, Pallas kernels: none -> 468 us  [the longest x6 157 us: call_a(): pl.pallas_call(functools.partial(stage_a, heads), grid=(pairs,), in_specs...]
    dot_general x27 -> x0, matrix products: 447 us -> none  [the longest x6 96.2 us: project_qkv(): jnp.einsum('...d,dshe->...she', normed, w_qkv, preferred_element_type=jnp...]
    ppermute x6 -> x12, waiting for transfers between devices: 289 us -> 5.87 us  [the longest x6 5.85 us: step(): from_next = lax.ppermute(updated[0], 'frames', to_prev)]
    concatenate x6 -> x0, local copies, waits for them, and re-layouts: 212 us -> none  [the longest x3 106 us: temporal_mix(): jnp.concatenate([halo[..., 1, :, :], projected[..., 2, :, :]], axis=-4)]
    sub x6 -> x0, matrix products: 160 us -> none  [the longest x3 84.8 us: temporal_mix(): attn_probs = jax.nn.softmax(scores, axis=-1).astype(jnp.bfloat16)]
    squeeze x14 -> x1, local copies, waits for them, and re-layouts: 98.9 us -> 0.08 us  [local(): tm_bias[0]]
    reduce_sum x12 -> x0, other arithmetic: 49.3 us -> none  [layer_norm(): variance = jnp.mean(centered * centered, axis=-1, keepdims=True)]
    concatenate x6, other arithmetic: 33.4 us -> 0.1 us  [step(): new.append(jnp.concatenate([updated[1:], incoming[None]], axis=0))]
  transfers between devices with their start and end apart: 7 -> 13, of which waited for: 4 -> 4; matrix products, arithmetic and copies ran while one was open for 6% -> 5% of each run, Pallas kernels for 0% -> 61%
where the time goes in v1:
time: 643 us; the launch traced here: 641 us
  Pallas kernels  468 us (73%)
  waiting for transfers between devices  68.8 us (11%)
  local copies, waits for them, and re-layouts  52.4 us (8%)
  starting transfers between devices  36.6 us (6%)
  between operations  14.2 us (2%)
    pallas_call x6, Pallas kernels, call_a(): pl.pallas_call(functools.partial(stage_a, heads), grid=(pairs,), in_specs...  157 us
    pallas_call x6, Pallas kernels, call_m(): pl.pallas_call(stage_m, grid=(pairs,), in_specs=[pair_block(), pair_block...  156 us
    pallas_call x6, Pallas kernels, call_t(): pl.pallas_call(functools.partial(stage_t, heads), grid=(tokens // 16,), i...  155 us
    unnamed x2, waiting for transfers between devices  62.9 us
    ppermute x6, starting transfers between devices, step(): halos = [lax.ppermute(front[n][1], 'frames', to_next) for n in range(2)]  28.7 us
    slice x15, local copies, waits for them, and re-layouts, step(): new.append(jnp.concatenate([updated[1:], incoming[None]], axis=0))  13.1 us
  transfers between devices with their start and end apart: 13, of which 4 were waited for; matrix products, arithmetic and copies ran while one was open for 5% of the time, Pallas kernels for 61%

profile of v1, /device:TPU:22, one launch (start us, length us, event | category | flops | bytes accessed | tf_op | source)
XLA Modules:
  0.0 641.4 jit_solution(6411191790197149540)
XLA Ops:
  7.3 0.9 copy.64
  8.2 0.9 copy.65
  9.1 2.4 copy.59
  11.5 1.5 copy.60
  13.3 1.0 gather_fusion
  15.0 0.7 copy_bitcast_fusion
  15.7 551.0 %while.18 = (s32[]{:T(128)}, f32[16,256,4]{1,0,2:T(8,128)S(1)}, f32[16,256,4]{1,0,2:T(8,128)S(1)}, f32[3,2,256,4]{2,3,1,0:T(4,128)S(1)}, f32[16,6,384]{2,1,0:T(8...) while((s32[]{:T(128)}, f32[16,256,4]{1,0,2:T(8,128)S(1)}, ...), condition=%wide.region_1.2_spmd.clone.clone, body=%wide.region_0.1_spmd.clone.sunk.clone | while | flops 120000028672 | bytes 103363496 | solution.py:227
  15.8 2.1 copy.105.z_ref
  17.8 26.2 %stage_a.6 = (bf16[8,512,384]{2,1,0:T(8,128)(2,1)}, bf16[8,512,384]{2,1,0:T(8,128)(2,1)}) custom-call(f32[16,256,4]{2,1,0:T(8,128)} %copy.105.z_ref, f32[16,6,384]{2,1,0:T(8,128)} %get-tuple-element.624.mod_ref, bf16[4,384]{1,0:T(4,128)(2,1)S(1)} %get-tuple-element.625.w_in, bf16[1152,384]{1,0:T(8,128)(2,1)} %get-tuple-element.626.wqkv_t, ...), custom_call_target="tpu_custom_call" | custom-call | flops 20000000000 | bytes 12000000 | tf_op jit(solution)/shard_map/while/body/eval_jaxpr/stage_a/pallas_call | solution.py:186
  44.0 3.5 collective-permute-start
  47.5 2.0 copy.109.z_ref
  49.5 26.1 %stage_a.7 = (bf16[8,512,384]{2,1,0:T(8,128)(2,1)}, bf16[8,512,384]{2,1,0:T(8,128)(2,1)}) custom-call(f32[16,256,4]{2,1,0:T(8,128)} %copy.109.z_ref, f32[16,6,384]{2,1,0:T(8,128)S(1)} %get-tuple-element.636.mod_ref, bf16[4,384]{1,0:T(4,128)(2,1)S(1)} %get-tuple-element.625.w_in, bf16[1152,384]{1,0:T(8,128)(2,1)} %get-tuple-element.626.wqkv_t, ...), custom_call_target="tpu_custom_call" | custom-call | flops 20000000000 | bytes 12000000 | tf_op jit(solution)/shard_map/while/body/eval_jaxpr/stage_a/pallas_call | solution.py:186
  75.6 4.3 collective-permute-start.2
  81.6 0.9 broadcast_in_dim.75.bias_ref
  82.5 25.8 %stage_t.2.o_ref = bf16[8,512,384]{2,1,0:T(8,128)(2,1)} custom-call(bf16[8,512,384]{2,1,0:T(8,128)(2,1)} %collective-permute-done.halo_ref, bf16[8,512,384]{2,1,0:T(8,128)(2,1)} %get-tuple-element.551.own_ref, bf16[1152,384]{1,0:T(8,128)(2,1)} %get-tuple-element.628.wqkv_t, f32[32,8,768]{2,1,0:T(8,128)} %broadcast_in_dim.75.bias_ref), custom_call_target="tpu_custom_call" | custom-call | flops 20000000000 | bytes 12000000 | tf_op jit(solution)/shard_map/while/body/eval_jaxpr/stage_t/pallas_call | solution.py:195
  108.3 26.0 %stage_m.6 = f32[16,256,4]{2,1,0:T(8,128)} custom-call(bf16[8,512,384]{2,1,0:T(8,128)(2,1)} %stage_t.2.o_ref, bf16[8,512,384]{2,1,0:T(8,128)(2,1)} %get-tuple-element.552.x_ref, f32[16,6,384]{2,1,0:T(8,128)} %get-tuple-element.624.mod_ref, f32[16]{0:T(128)S(1)} %get-tuple-element.629.dt_ref, f32[16,256,4]{2,1,0:T(8,128)} %copy.105.z_ref, ...), custom_call_target="tpu_custom_call" | custom-call | flops 20000000000 | bytes 12000000 | tf_op jit(solution)/shard_map/while/body/eval_jaxpr/stage_m/pallas_call | solution.py:203
  134.4 0.9 fusion.25
  135.3 1.3 collective-permute-start.1
  136.6 25.9 %stage_t.3.o_ref = bf16[8,512,384]{2,1,0:T(8,128)(2,1)} custom-call(bf16[8,512,384]{2,1,0:T(8,128)(2,1)} %collective-permute-done.2.halo_ref, bf16[8,512,384]{2,1,0:T(8,128)(2,1)} %get-tuple-element.554.own_ref, bf16[1152,384]{1,0:T(8,128)(2,1)} %get-tuple-element.628.wqkv_t, f32[32,8,768]{2,1,0:T(8,128)} %broadcast_in_dim.75.bias_ref), custom_call_target="tpu_custom_call" | custom-call | flops 20000000000 | bytes 12000000 | tf_op jit(solution)/shard_map/while/body/eval_jaxpr/stage_t/pallas_call | solution.py:195
  162.5 26.1 %stage_m.7 = f32[16,256,4]{2,1,0:T(8,128)} custom-call(bf16[8,512,384]{2,1,0:T(8,128)(2,1)} %stage_t.3.o_ref, bf16[8,512,384]{2,1,0:T(8,128)(2,1)} %get-tuple-element.555.x_ref, f32[16,6,384]{2,1,0:T(8,128)S(1)} %get-tuple-element.636.mod_ref, f32[16]{0:T(128)S(1)} %get-tuple-element.637.dt_ref, f32[16,256,4]{2,1,0:T(8,128)} %copy.109.z_ref, ...), custom_call_target="tpu_custom_call" | custom-call | flops 20000000000 | bytes 12000000 | tf_op jit(solution)/shard_map/while/body/eval_jaxpr/stage_m/pallas_call | solution.py:203
  188.6 0.9 fusion.27
  189.7 1.4 slice.58
  191.1 2.3 copy.108
  193.5 1.3 collective-permute-start.3
  195.5 2.1 collective-permute-done.3
  197.8 2.1 copy.105.z_ref
  199.8 26.2 %stage_a.6 = (bf16[8,512,384]{2,1,0:T(8,128)(2,1)}, bf16[8,512,384]{2,1,0:T(8,128)(2,1)}) custom-call(f32[16,256,4]{2,1,0:T(8,128)} %copy.105.z_ref, f32[16,6,384]{2,1,0:T(8,128)} %get-tuple-element.624.mod_ref, bf16[4,384]{1,0:T(4,128)(2,1)S(1)} %get-tuple-element.625.w_in, bf16[1152,384]{1,0:T(8,128)(2,1)} %get-tuple-element.626.wqkv_t, ...), custom_call_target="tpu_custom_call" | custom-call | flops 20000000000 | bytes 12000000 | tf_op jit(solution)/shard_map/while/body/eval_jaxpr/stage_a/pallas_call | solution.py:186
  226.0 7.9 %collective-permute-start = (bf16[8,512,384]{2,1,0:T(8,128)(2,1)}, bf16[8,512,384]{2,1,0:T(8,128)(2,1)}, u32[]{:S(2)}, u32[]{:S(2)}) collective-permute-start(bf16[8,512,384]{2,1,0:T(8,128)(2,1)} %get-tuple-element.551.own_ref), channel_id=1, source_target_pairs={{0,1},{1,2},{2,3},{3,4},{4,5},{5,6},{6,7},{7,8},{8,9},{9,10},{10,1... | collective-permute-start | bytes 9437192 | tf_op jit(solution)/shard_map/while/body/eval_jaxpr/ppermute | solution.py:216
  233.9 2.0 copy.109.z_ref
  235.9 26.1 %stage_a.7 = (bf16[8,512,384]{2,1,0:T(8,128)(2,1)}, bf16[8,512,384]{2,1,0:T(8,128)(2,1)}) custom-call(f32[16,256,4]{2,1,0:T(8,128)} %copy.109.z_ref, f32[16,6,384]{2,1,0:T(8,128)S(1)} %get-tuple-element.636.mod_ref, bf16[4,384]{1,0:T(4,128)(2,1)S(1)} %get-tuple-element.625.w_in, bf16[1152,384]{1,0:T(8,128)(2,1)} %get-tuple-element.626.wqkv_t, ...), custom_call_target="tpu_custom_call" | custom-call | flops 20000000000 | bytes 12000000 | tf_op jit(solution)/shard_map/while/body/eval_jaxpr/stage_a/pallas_call | solution.py:186
  262.0 3.0 collective-permute-start.2
  266.7 0.9 broadcast_in_dim.75.bias_ref
  267.6 25.8 %stage_t.2.o_ref = bf16[8,512,384]{2,1,0:T(8,128)(2,1)} custom-call(bf16[8,512,384]{2,1,0:T(8,128)(2,1)} %collective-permute-done.halo_ref, bf16[8,512,384]{2,1,0:T(8,128)(2,1)} %get-tuple-element.551.own_ref, bf16[1152,384]{1,0:T(8,128)(2,1)} %get-tuple-element.628.wqkv_t, f32[32,8,768]{2,1,0:T(8,128)} %broadcast_in_dim.75.bias_ref), custom_call_target="tpu_custom_call" | custom-call | flops 20000000000 | bytes 12000000 | tf_op jit(solution)/shard_map/while/body/eval_jaxpr/stage_t/pallas_call | solution.py:195
  293.5 26.0 %stage_m.6 = f32[16,256,4]{2,1,0:T(8,128)} custom-call(bf16[8,512,384]{2,1,0:T(8,128)(2,1)} %stage_t.2.o_ref, bf16[8,512,384]{2,1,0:T(8,128)(2,1)} %get-tuple-element.552.x_ref, f32[16,6,384]{2,1,0:T(8,128)} %get-tuple-element.624.mod_ref, f32[16]{0:T(128)S(1)} %get-tuple-element.629.dt_ref, f32[16,256,4]{2,1,0:T(8,128)} %copy.105.z_ref, ...), custom_call_target="tpu_custom_call" | custom-call | flops 20000000000 | bytes 12000000 | tf_op jit(solution)/shard_map/while/body/eval_jaxpr/stage_m/pallas_call | solution.py:203
  319.5 0.9 fusion.25
  320.4 1.3 collective-permute-start.1
  321.8 25.9 %stage_t.3.o_ref = bf16[8,512,384]{2,1,0:T(8,128)(2,1)} custom-call(bf16[8,512,384]{2,1,0:T(8,128)(2,1)} %collective-permute-done.2.halo_ref, bf16[8,512,384]{2,1,0:T(8,128)(2,1)} %get-tuple-element.554.own_ref, bf16[1152,384]{1,0:T(8,128)(2,1)} %get-tuple-element.628.wqkv_t, f32[32,8,768]{2,1,0:T(8,128)} %broadcast_in_dim.75.bias_ref), custom_call_target="tpu_custom_call" | custom-call | flops 20000000000 | bytes 12000000 | tf_op jit(solution)/shard_map/while/body/eval_jaxpr/stage_t/pallas_call | solution.py:195
  347.6 26.1 %stage_m.7 = f32[16,256,4]{2,1,0:T(8,128)} custom-call(bf16[8,512,384]{2,1,0:T(8,128)(2,1)} %stage_t.3.o_ref, bf16[8,512,384]{2,1,0:T(8,128)(2,1)} %get-tuple-element.555.x_ref, f32[16,6,384]{2,1,0:T(8,128)S(1)} %get-tuple-element.636.mod_ref, f32[16]{0:T(128)S(1)} %get-tuple-element.637.dt_ref, f32[16,256,4]{2,1,0:T(8,128)} %copy.109.z_ref, ...), custom_call_target="tpu_custom_call" | custom-call | flops 20000000000 | bytes 12000000 | tf_op jit(solution)/shard_map/while/body/eval_jaxpr/stage_m/pallas_call | solution.py:203
  373.7 0.9 fusion.27
  374.8 1.4 slice.58
  376.3 2.3 copy.108
  378.6 1.3 collective-permute-start.3
  380.6 1.9 collective-permute-done.3
  382.7 2.1 copy.105.z_ref
  384.7 26.2 %stage_a.6 = (bf16[8,512,384]{2,1,0:T(8,128)(2,1)}, bf16[8,512,384]{2,1,0:T(8,128)(2,1)}) custom-call(f32[16,256,4]{2,1,0:T(8,128)} %copy.105.z_ref, f32[16,6,384]{2,1,0:T(8,128)} %get-tuple-element.624.mod_ref, bf16[4,384]{1,0:T(4,128)(2,1)S(1)} %get-tuple-element.625.w_in, bf16[1152,384]{1,0:T(8,128)(2,1)} %get-tuple-element.626.wqkv_t, ...), custom_call_target="tpu_custom_call" | custom-call | flops 20000000000 | bytes 12000000 | tf_op jit(solution)/shard_map/while/body/eval_jaxpr/stage_a/pallas_call | solution.py:186
  410.9 7.2 %collective-permute-start = (bf16[8,512,384]{2,1,0:T(8,128)(2,1)}, bf16[8,512,384]{2,1,0:T(8,128)(2,1)}, u32[]{:S(2)}, u32[]{:S(2)}) collective-permute-start(bf16[8,512,384]{2,1,0:T(8,128)(2,1)} %get-tuple-element.551.own_ref), channel_id=1, source_target_pairs={{0,1},{1,2},{2,3},{3,4},{4,5},{5,6},{6,7},{7,8},{8,9},{9,10},{10,1... | collective-permute-start | bytes 9437192 | tf_op jit(solution)/shard_map/while/body/eval_jaxpr/ppermute | solution.py:216
  418.0 2.0 copy.109.z_ref
  420.0 26.1 %stage_a.7 = (bf16[8,512,384]{2,1,0:T(8,128)(2,1)}, bf16[8,512,384]{2,1,0:T(8,128)(2,1)}) custom-call(f32[16,256,4]{2,1,0:T(8,128)} %copy.109.z_ref, f32[16,6,384]{2,1,0:T(8,128)S(1)} %get-tuple-element.636.mod_ref, bf16[4,384]{1,0:T(4,128)(2,1)S(1)} %get-tuple-element.625.w_in, bf16[1152,384]{1,0:T(8,128)(2,1)} %get-tuple-element.626.wqkv_t, ...), custom_call_target="tpu_custom_call" | custom-call | flops 20000000000 | bytes 12000000 | tf_op jit(solution)/shard_map/while/body/eval_jaxpr/stage_a/pallas_call | solution.py:186
  446.2 3.0 collective-permute-start.2
  450.8 0.9 broadcast_in_dim.75.bias_ref
  451.8 25.8 %stage_t.2.o_ref = bf16[8,512,384]{2,1,0:T(8,128)(2,1)} custom-call(bf16[8,512,384]{2,1,0:T(8,128)(2,1)} %collective-permute-done.halo_ref, bf16[8,512,384]{2,1,0:T(8,128)(2,1)} %get-tuple-element.551.own_ref, bf16[1152,384]{1,0:T(8,128)(2,1)} %get-tuple-element.628.wqkv_t, f32[32,8,768]{2,1,0:T(8,128)} %broadcast_in_dim.75.bias_ref), custom_call_target="tpu_custom_call" | custom-call | flops 20000000000 | bytes 12000000 | tf_op jit(solution)/shard_map/while/body/eval_jaxpr/stage_t/pallas_call | solution.py:195
  477.6 26.0 %stage_m.6 = f32[16,256,4]{2,1,0:T(8,128)} custom-call(bf16[8,512,384]{2,1,0:T(8,128)(2,1)} %stage_t.2.o_ref, bf16[8,512,384]{2,1,0:T(8,128)(2,1)} %get-tuple-element.552.x_ref, f32[16,6,384]{2,1,0:T(8,128)} %get-tuple-element.624.mod_ref, f32[16]{0:T(128)S(1)} %get-tuple-element.629.dt_ref, f32[16,256,4]{2,1,0:T(8,128)} %copy.105.z_ref, ...), custom_call_target="tpu_custom_call" | custom-call | flops 20000000000 | bytes 12000000 | tf_op jit(solution)/shard_map/while/body/eval_jaxpr/stage_m/pallas_call | solution.py:203
  503.6 0.9 fusion.25
  504.6 1.3 collective-permute-start.1
  505.9 25.9 %stage_t.3.o_ref = bf16[8,512,384]{2,1,0:T(8,128)(2,1)} custom-call(bf16[8,512,384]{2,1,0:T(8,128)(2,1)} %collective-permute-done.2.halo_ref, bf16[8,512,384]{2,1,0:T(8,128)(2,1)} %get-tuple-element.554.own_ref, bf16[1152,384]{1,0:T(8,128)(2,1)} %get-tuple-element.628.wqkv_t, f32[32,8,768]{2,1,0:T(8,128)} %broadcast_in_dim.75.bias_ref), custom_call_target="tpu_custom_call" | custom-call | flops 20000000000 | bytes 12000000 | tf_op jit(solution)/shard_map/while/body/eval_jaxpr/stage_t/pallas_call | solution.py:195
  531.7 26.1 %stage_m.7 = f32[16,256,4]{2,1,0:T(8,128)} custom-call(bf16[8,512,384]{2,1,0:T(8,128)(2,1)} %stage_t.3.o_ref, bf16[8,512,384]{2,1,0:T(8,128)(2,1)} %get-tuple-element.555.x_ref, f32[16,6,384]{2,1,0:T(8,128)S(1)} %get-tuple-element.636.mod_ref, f32[16]{0:T(128)S(1)} %get-tuple-element.637.dt_ref, f32[16,256,4]{2,1,0:T(8,128)} %copy.109.z_ref, ...), custom_call_target="tpu_custom_call" | custom-call | flops 20000000000 | bytes 12000000 | tf_op jit(solution)/shard_map/while/body/eval_jaxpr/stage_m/pallas_call | solution.py:203
  557.8 0.9 fusion.27
  558.9 1.4 slice.58
  560.4 2.3 copy.108
  562.7 1.3 collective-permute-start.3
  564.8 1.9 collective-permute-done.3
  567.2 0.9 reshape.133
  569.5 62.8 %reduce-scatter.4.cloned.1.call-done = f32[16,24]{1,0:T(8,128)} async-done(((f32[256,24]{1,0:T(8,128)}), f32[16,24]{1,0:T(8,128)}) %reduce-scatter.4.cloned.1.call-update) | async-done | bytes 1552
  632.4 0.8 reshape.134
  (102 shorter events, 12.2 us)
Async XLA Ops:
  7.2 4.3 copy-start.1
  7.2 625.2 %reduce-scatter.4.cloned.1.call-start = ((), (), s32[]{:S(2)}) async-start(), calls=%async_computation.1 | async-start | bytes 139264
  9.1 4.0 copy-start.4
  11.5 3.4 copy-start.2
  11.5 3.4 copy-start.3
  13.0 2.7 copy-start.5
  13.0 2.7 copy-start.6
  13.0 2.7 copy-start.7
  13.0 2.7 copy-start.8
  44.0 37.6 %collective-permute-start = (bf16[8,512,384]{2,1,0:T(8,128)(2,1)}, bf16[8,512,384]{2,1,0:T(8,128)(2,1)}, u32[]{:S(2)}, u32[]{:S(2)}) collective-permute-start(bf16[8,512,384]{2,1,0:T(8,128)(2,1)} %get-tuple-element.551.own_ref), channel_id=1, source_target_pairs={{0,1},{1,2},{2,3},{3,4},{4,5},{5,6},{6,7},{7,8},{8,9},{9,10},{10,1... | collective-permute-start | bytes 9437192 | tf_op jit(solution)/shard_map/while/body/eval_jaxpr/ppermute | solution.py:216
  75.6 61.0 %collective-permute-start.2 = (bf16[8,512,384]{2,1,0:T(8,128)(2,1)}, bf16[8,512,384]{2,1,0:T(8,128)(2,1)}, u32[]{:S(2)}, u32[]{:S(2)}) collective-permute-start(bf16[8,512,384]{2,1,0:T(8,128)(2,1)} %get-tuple-element.554.own_ref), channel_id=1, source_target_pairs={{0,1},{1,2},{2,3},{3,4},{4,5},{5,6},{6,7},{7,8},{8,9},{9,10},{10,1... | collective-permute-start | bytes 9437192 | tf_op jit(solution)/shard_map/while/body/eval_jaxpr/ppermute | solution.py:216
  135.3 60.1 %collective-permute-start.1 = (f32[256,4]{1,0:T(8,128)S(1)}, f32[256,4]{1,0:T(8,128)S(1)}, u32[]{:S(2)}, u32[]{:S(2)}) collective-permute-start(f32[256,4]{1,0:T(8,128)S(1)} %get-tuple-element.553), channel_id=1, source_target_pairs={{1,0},{2,1},{3,2},{4,3},{5,4},{6,5},{7,6},{8,7},{9,8},{10,9},{11,1... | collective-permute-start | bytes 12296 | tf_op jit(solution)/shard_map/while/body/eval_jaxpr/ppermute | solution.py:221
  162.5 27.2 %copy-start = (f32[16,256,4]{2,1,0:T(8,128)S(1)}, f32[16,256,4]{2,1,0:T(8,128)}, u32[]{:S(2)}) copy-start(f32[16,256,4]{2,1,0:T(8,128)} %stage_m.6) | copy-start | bytes 196612 | tf_op jit(solution)/shard_map/while
  191.1 3.6 slice-start
  193.5 4.2 collective-permute-start.3
  226.0 40.7 %collective-permute-start = (bf16[8,512,384]{2,1,0:T(8,128)(2,1)}, bf16[8,512,384]{2,1,0:T(8,128)(2,1)}, u32[]{:S(2)}, u32[]{:S(2)}) collective-permute-start(bf16[8,512,384]{2,1,0:T(8,128)(2,1)} %get-tuple-element.551.own_ref), channel_id=1, source_target_pairs={{0,1},{1,2},{2,3},{3,4},{4,5},{5,6},{6,7},{7,8},{8,9},{9,10},{10,1... | collective-permute-start | bytes 9437192 | tf_op jit(solution)/shard_map/while/body/eval_jaxpr/ppermute | solution.py:216
  262.0 59.7 %collective-permute-start.2 = (bf16[8,512,384]{2,1,0:T(8,128)(2,1)}, bf16[8,512,384]{2,1,0:T(8,128)(2,1)}, u32[]{:S(2)}, u32[]{:S(2)}) collective-permute-start(bf16[8,512,384]{2,1,0:T(8,128)(2,1)} %get-tuple-element.554.own_ref), channel_id=1, source_target_pairs={{0,1},{1,2},{2,3},{3,4},{4,5},{5,6},{6,7},{7,8},{8,9},{9,10},{10,1... | collective-permute-start | bytes 9437192 | tf_op jit(solution)/shard_map/while/body/eval_jaxpr/ppermute | solution.py:216
  320.4 60.1 %collective-permute-start.1 = (f32[256,4]{1,0:T(8,128)S(1)}, f32[256,4]{1,0:T(8,128)S(1)}, u32[]{:S(2)}, u32[]{:S(2)}) collective-permute-start(f32[256,4]{1,0:T(8,128)S(1)} %get-tuple-element.553), channel_id=1, source_target_pairs={{1,0},{2,1},{3,2},{4,3},{5,4},{6,5},{7,6},{8,7},{9,8},{10,9},{11,1... | collective-permute-start | bytes 12296 | tf_op jit(solution)/shard_map/while/body/eval_jaxpr/ppermute | solution.py:221
  347.6 27.2 %copy-start = (f32[16,256,4]{2,1,0:T(8,128)S(1)}, f32[16,256,4]{2,1,0:T(8,128)}, u32[]{:S(2)}) copy-start(f32[16,256,4]{2,1,0:T(8,128)} %stage_m.6) | copy-start | bytes 196612 | tf_op jit(solution)/shard_map/while
  376.3 3.6 slice-start
  378.6 3.9 collective-permute-start.3
  410.9 39.9 %collective-permute-start = (bf16[8,512,384]{2,1,0:T(8,128)(2,1)}, bf16[8,512,384]{2,1,0:T(8,128)(2,1)}, u32[]{:S(2)}, u32[]{:S(2)}) collective-permute-start(bf16[8,512,384]{2,1,0:T(8,128)(2,1)} %get-tuple-element.551.own_ref), channel_id=1, source_target_pairs={{0,1},{1,2},{2,3},{3,4},{4,5},{5,6},{6,7},{7,8},{8,9},{9,10},{10,1... | collective-permute-start | bytes 9437192 | tf_op jit(solution)/shard_map/while/body/eval_jaxpr/ppermute | solution.py:216
  446.2 59.7 %collective-permute-start.2 = (bf16[8,512,384]{2,1,0:T(8,128)(2,1)}, bf16[8,512,384]{2,1,0:T(8,128)(2,1)}, u32[]{:S(2)}, u32[]{:S(2)}) collective-permute-start(bf16[8,512,384]{2,1,0:T(8,128)(2,1)} %get-tuple-element.554.own_ref), channel_id=1, source_target_pairs={{0,1},{1,2},{2,3},{3,4},{4,5},{5,6},{6,7},{7,8},{8,9},{9,10},{10,1... | collective-permute-start | bytes 9437192 | tf_op jit(solution)/shard_map/while/body/eval_jaxpr/ppermute | solution.py:216
  504.6 60.1 %collective-permute-start.1 = (f32[256,4]{1,0:T(8,128)S(1)}, f32[256,4]{1,0:T(8,128)S(1)}, u32[]{:S(2)}, u32[]{:S(2)}) collective-permute-start(f32[256,4]{1,0:T(8,128)S(1)} %get-tuple-element.553), channel_id=1, source_target_pairs={{1,0},{2,1},{3,2},{4,3},{5,4},{6,5},{7,6},{8,7},{9,8},{10,9},{11,1... | collective-permute-start | bytes 12296 | tf_op jit(solution)/shard_map/while/body/eval_jaxpr/ppermute | solution.py:221
  531.7 27.2 %copy-start = (f32[16,256,4]{2,1,0:T(8,128)S(1)}, f32[16,256,4]{2,1,0:T(8,128)}, u32[]{:S(2)}) copy-start(f32[16,256,4]{2,1,0:T(8,128)} %stage_m.6) | copy-start | bytes 196612 | tf_op jit(solution)/shard_map/while
  560.4 3.6 slice-start
  562.7 3.9 collective-permute-start.3
Sparse Core Ops, SparseCore 0:
  568.3 64.0 reduce-scatter.3

commit v2 on v1

v2 whole, which is shorter than its diff:
```python
import functools
import jax
import jax.numpy as jnp
from jax import lax
from jax.experimental import pallas as pl
from jax.experimental.pallas import tpu as pltpu
from jax.sharding import PartitionSpec as P

LN_EPS = 1e-6
MASKED = -1e30
LOG2E = 1.4426950408889634
F32 = jnp.float32
BF16 = jnp.bfloat16


def mm(lhs, rhs, lc, rc):
    return lax.dot_general(lhs, rhs, (((lc,), (rc,)), ((), ())), preferred_element_type=F32)


def norm(x, axis):
    centered = x - jnp.mean(x, axis=axis, keepdims=True)
    return centered * lax.rsqrt(jnp.mean(centered * centered, axis=axis, keepdims=True) + LN_EPS)


def pipelined(items, scores, weigh, mix, ahead=2, behind=2):
    raw, weighed = {}, {}
    count = len(items)
    for n in range(-ahead, count + behind):
        if n + ahead < count:
            raw[n + ahead] = scores(items[n + ahead])
        if 0 <= n < count:
            weighed[n] = weigh(items[n], raw.pop(n))
        if 0 <= n - behind < count:
            mix(items[n - behind], weighed.pop(n - behind))


def spatial(u, wqkv_t, wo, heads):
    rows, dim = u.shape
    half = rows // 2
    width = dim // heads
    qkv = mm(wqkv_t, u, 1, 1).astype(BF16)
    outs = {}

    def part(index, h, f):
        return qkv[index * dim + h * width:index * dim + (h + 1) * width, f * half:(f + 1) * half]

    items = [(h, f) for h in range(heads) for f in range(2)]
    keys = {item: part(1, *item).T for item in items}

    def scores(item):
        return mm(keys[item], part(0, *item), 1, 0)

    def weigh(item, s):
        p = jnp.exp2((s - jnp.max(s, axis=0, keepdims=True)) * (LOG2E * width ** -0.5))
        return p.astype(BF16), 1.0 / jnp.sum(p, axis=0, keepdims=True)

    def mix(item, weighed):
        outs[item] = (mm(part(2, *item), weighed[0], 1, 0) * weighed[1]).astype(BF16)

    pipelined(items, scores, weigh, mix)
    mixed = jnp.concatenate([jnp.concatenate([outs[h, f] for f in range(2)], axis=1) for h in range(heads)], axis=0)
    return mm(mixed, wo, 0, 0)


def pair_rows(first, second):
    rows, dim = first.shape
    both = jnp.concatenate([first.reshape(rows // 8, 1, 8, dim), second.reshape(rows // 8, 1, 8, dim)], axis=1)
    return both.reshape(2 * rows, dim)


def pair_mod(x, scale, shift):
    rows, dim = x.shape
    x = x.reshape(rows // 16, 2, 8, dim)
    return (x * scale[None, :, None, :] + shift[None, :, None, :]).reshape(rows, dim)


def stage_a(z, mod, w_in, wqkv_t, wo, heads):
    rows = z.shape[0] // 2
    x0 = mm(z.astype(BF16), w_in, 1, 0).astype(BF16).astype(F32)
    n0 = norm(x0, -1)
    u = jnp.concatenate([n0[s * rows:(s + 1) * rows] * mod[s, 1:2] + mod[s, 0:1] for s in range(2)], axis=0).astype(BF16)
    x = x0 + spatial(u, wqkv_t, wo, heads)
    x = pair_rows(x[:rows], x[rows:]).astype(BF16)
    return x, pair_mod(norm(x.astype(F32), -1), mod[:, 3], mod[:, 2]).astype(BF16)


def stage_t(us, wqkv_t, bias_ref, heads):
    keys, dim = us[0].shape
    groups = len(us)
    queries = keys // 2
    width = dim // heads
    q_all = (mm(wqkv_t[:dim], jnp.concatenate([u[queries:] for u in us], axis=0), 1, 1) * width ** -0.5).astype(BF16)
    kv_all = mm(wqkv_t[dim:], jnp.concatenate(us, axis=0), 1, 1).astype(BF16)
    sub = lax.broadcasted_iota(jnp.int32, (keys, 2 * queries), 0) % 8
    lane = lax.broadcasted_iota(jnp.int32, (keys, 2 * queries), 1) % 8
    same = sub == lane
    outs = {}
    items = [(pair, g) for pair in range(heads // 2) for g in range(groups)]
    rows = lambda pair: slice(2 * pair * width, 2 * (pair + 1) * width)
    k_rows = {(pair, g): kv_all[rows(pair), g * keys:(g + 1) * keys].T for pair, g in items}
    zero = jnp.zeros((width, queries), BF16)

    def scores(item):
        pair, g = item
        q = q_all[rows(pair), g * queries:(g + 1) * queries]
        q = jnp.concatenate([jnp.concatenate([q[:width], zero], axis=1), jnp.concatenate([zero, q[width:]], axis=1)], axis=0)
        return mm(k_rows[item], q, 1, 0)

    def weigh(item, s):
        pair, g = item
        s = s.reshape(keys // 8, 8, 2 * queries) + bias_ref[:, :, 2 * pair * queries:2 * (pair + 1) * queries]
        p = jnp.exp2((s - jnp.max(s, axis=0, keepdims=True)) * LOG2E)
        total = jnp.sum(p, axis=0)
        total = jnp.sum(jnp.where(same[:8], total, 0.0), axis=0, keepdims=True)
        return jnp.where(same, p.reshape(keys, 2 * queries), 0.0).astype(BF16), 1.0 / total

    def mix(item, weighed):
        pair, g = item
        mixed = mm(kv_all[dim + 2 * pair * width:dim + 2 * (pair + 1) * width, g * keys:(g + 1) * keys], weighed[0], 1, 0) * weighed[1]
        outs[item] = jnp.concatenate([mixed[:width, :queries], mixed[width:, queries:]], axis=0).astype(BF16)

    pipelined(items, scores, weigh, mix)
    return [jnp.concatenate([outs[pair, g] for pair in range(heads // 2)], axis=0).T for g in range(groups)]


def stage_m(o, x, mod, wo, w_up_t, w_down_t, w_out_t):
    x = (x.astype(F32) + mm(o, wo, 1, 0)).astype(BF16)
    u = pair_mod(norm(x.astype(F32), -1), mod[:, 5], mod[:, 4]).astype(BF16)
    tokens = x.shape[0] // 2
    h = mm(w_up_t, u, 1, 1)
    t = jnp.tanh(h * (1.5957691216057308 + 0.285419265090401 * (h * h)))
    h = (h + h * t).astype(BF16)
    x_t = (x.T.astype(F32) + mm(w_down_t, h, 1, 0)).astype(BF16).astype(F32)
    v = mm(w_out_t, norm(x_t, 0).astype(BF16), 1, 0)[:8].T.reshape(tokens // 8, 2, 8, 8)
    return [v[:, s].reshape(tokens, 8) for s in range(2)]


def kernel(group, heads, lat_a, lat_b, noise_a, noise_b, mod_a, mod_b, dt_a, dt_b, table, w_in, sp_t, sp_o, tm_t, tm_o, up_t, down_t, out_t,
           fin_a, fin_b, emit_a, emit_b,
           z_buf, z_in, z_noise, mod_buf, dt_buf, x_buf, u_buf, o_buf, e_buf,
           send_sem, recv_sem, free_sem, z_send, z_recv, e_send, e_recv):
    slots, channels, tokens = lat_a.shape
    steps = noise_a.shape[0]
    pairs = slots // 2
    me = lax.axis_index('frames')
    last = group - 1
    nxt = jnp.minimum(me + 1, last)
    prv = jnp.maximum(me - 1, 0)
    mesh_id = pl.DeviceIdType.MESH
    share = tokens // group

    def halo_copy(n, f):
        return pltpu.make_async_remote_copy(
            src_ref=u_buf.at[n, pairs + f], dst_ref=u_buf.at[n, f], send_sem=send_sem.at[n, f], recv_sem=recv_sem.at[n, f],
            device_id={'frames': nxt}, device_id_type=mesh_id)

    def z_copy(n):
        return pltpu.make_async_remote_copy(
            src_ref=z_buf.at[n, slots], dst_ref=z_in.at[n], send_sem=z_send.at[n], recv_sem=z_recv.at[n],
            device_id={'frames': prv}, device_id_type=mesh_id)

    def e_copy(n, t, d):
        return pltpu.make_async_remote_copy(
            src_ref=z_buf.at[n, slots, pl.ds(pl.multiple_of(d * share, 8), share)], dst_ref=e_buf.at[n, t],
            send_sem=e_send.at[n, d], recv_sem=e_recv.at[n, t], device_id={'frames': d}, device_id_type=mesh_id)

    barrier = pltpu.get_barrier_semaphore()

    @pl.when(me > 0)
    def _():
        pl.semaphore_signal(barrier, inc=1, device_id={'frames': prv}, device_id_type=mesh_id)

    @pl.when(me > 1)
    def _():
        pl.semaphore_signal(barrier, inc=1, device_id={'frames': 0}, device_id_type=mesh_id)

    @pl.when(me < last)
    def _():
        pl.semaphore_signal(barrier, inc=1, device_id={'frames': nxt}, device_id_type=mesh_id)

    for n, (lat, mod, dt, noise) in enumerate(((lat_a, mod_a, dt_a, noise_a), (lat_b, mod_b, dt_b, noise_b))):
        @pl.loop(0, slots)
        def _(k):
            z_buf[n, k] = lat[k].T
            m = mod[k]
            odd = lax.broadcasted_iota(jnp.int32, m.shape, 0) % 2
            m = jnp.where(odd == 1, 1.0 + m, m)
            mod_buf[n, k] = jnp.where(lax.broadcasted_iota(jnp.int32, m.shape, 0) >= 4, 0.5 * m, m)
            dt_buf[n, k] = dt[k]

        @pl.loop(0, steps)
        def _(t):
            z_noise[n, t] = noise[t].T

    @pl.when(me == 0)
    def _():
        @pl.loop(0, pairs)
        def _(f):
            for n in range(2):
                u_buf[n, f] = jnp.zeros(u_buf.shape[2:], BF16)

    pl.semaphore_wait(barrier, jnp.where(me == 0, last, jnp.where(me == last, 1, 2)))

    @pl.loop(0, steps)
    def _(t):
        @pl.loop(0, 2)
        def _(n):
            @pl.when((t > 0) & (me < last))
            def _():
                z_copy(n).wait_recv()
                z_buf[n, slots - 1] = z_in[n]

            @pl.when((t > 0) & (me == last))
            def _():
                z_buf[n, slots - 1] = z_noise[n, t - 1]

            @pl.when((t > 0) & (me < last))
            def _():
                pl.semaphore_wait(free_sem.at[n], 1)

            @pl.loop(0, pairs)
            def _(f):
                @pl.when((t > 0) & (me < last))
                def _():
                    halo_copy(n, f).wait_send()

                z = jnp.concatenate([z_buf[n, 2 * f], z_buf[n, 2 * f + 1]], axis=0)
                x, u = stage_a(z, mod_buf[n, pl.ds(2 * f, 2)], w_in[...], sp_t[...], sp_o[...], heads)
                x_buf[n, f] = x
                u_buf[n, pairs + f] = u

                @pl.when((f > 0) & (me < last))
                def _():
                    halo_copy(n, f - 1).start()

            @pl.when(me < last)
            def _():
                halo_copy(n, pairs - 1).start()

        @pl.loop(0, 2)
        def _(n):
            @pl.when(me > 0)
            def _():
                @pl.loop(0, pairs)
                def _(f):
                    halo_copy(n, f).wait_recv()

            @pl.loop(0, tokens // 16)
            def _(i):
                rows = pl.ds(pl.multiple_of(i * 32, 32), 32)
                both = u_buf[n, :, rows]
                mixed = stage_t([both[:, g * 16:(g + 1) * 16].reshape(-1, both.shape[-1]) for g in range(2)], tm_t, table, heads)
                o_buf[:, rows] = jnp.concatenate([m.reshape(pairs, 16, -1) for m in mixed], axis=1)

            @pl.when((t < steps - 1) & (me > 0))
            def _():
                pl.semaphore_signal(free_sem.at[n], inc=1, device_id={'frames': prv}, device_id_type=mesh_id)

            @pl.when((t > 0) & (me > 0))
            def _():
                z_copy(n).wait_send()

            @pl.when((t > 0) & (me == 0))
            def _():
                @pl.loop(1, group)
                def _(d):
                    e_copy(n, t - 1, d).wait_send()

            @pl.loop(0, pairs)
            def _(f):
                v = stage_m(o_buf[f], x_buf[n, f], mod_buf[n, pl.ds(2 * f, 2)], tm_o[...], up_t[...], down_t[...], out_t[...])
                new = [z_buf[n, 2 * f + s] + dt_buf[n, 2 * f + s] * v[s][:, :channels] for s in range(2)]
                z_buf[n, lax.rem(2 * f + slots, slots + 1)] = new[0]
                z_buf[n, 2 * f] = new[1]

                @pl.when((f == 1) & (me > 0))
                def _():
                    z_copy(n).start()

                @pl.when((f == 1) & (me == 0))
                def _():
                    e_buf[n, t] = z_buf[n, slots, :share]

                    @pl.loop(1, group)
                    def _(d):
                        e_copy(n, t, d).start()

    @pl.loop(0, 2)
    def _(n):
        @pl.when(me < last)
        def _():
            z_copy(n).wait_recv()
            z_buf[n, slots - 1] = z_in[n]

            @pl.loop(0, pairs)
            def _(f):
                halo_copy(n, f).wait_send()

        @pl.when(me == last)
        def _():
            z_buf[n, slots - 1] = z_noise[n, steps - 1]

        @pl.when(me > 0)
        def _():
            z_copy(n).wait_send()

            @pl.loop(0, steps)
            def _(t):
                e_copy(n, t, 0).wait_recv()

        @pl.when(me == 0)
        def _():
            @pl.loop(1, group)
            def _(d):
                e_copy(n, steps - 1, d).wait_send()

    for n, (fin, emit) in enumerate(((fin_a, emit_a), (fin_b, emit_b))):
        @pl.loop(0, slots)
        def _(k):
            fin[k] = z_buf[n, k].T

        emit[...] = e_buf[n]


def solution(mesh):
    group = mesh.shape['frames']
    slot_spec = P(('videos', 'frames'))
    emit_spec = P('videos', 'frames')
    whole = P()

    def local(latents_a, mod_a, dt_a, noise_a, latents_b, mod_b, dt_b, noise_b, w_in, sp_qkv, sp_out, tm_qkv, tm_bias, tm_out, mlp_up, mlp_down, w_out):
        position = lax.axis_index('frames')
        slots, tokens, channels = latents_a.shape
        steps = noise_a.shape[0]
        dim = w_in.shape[1]
        heads = tm_bias.shape[1]
        window = tm_bias.shape[-1]
        pairs = slots // 2
        sp_t = jnp.transpose(sp_qkv[0], (1, 2, 3, 0)).reshape(3 * dim, dim)
        tm_t = jnp.transpose(tm_qkv[0], (1, 2, 3, 0)).reshape(3 * dim, dim)
        out_t = jnp.pad(w_out.T, ((0, 16 - channels), (0, 0)))
        offset = jnp.arange(slots)[None, :] + slots - jnp.arange(2 * slots)[:, None]
        keep = (offset >= 0) & (offset < window) & ((jnp.arange(2 * slots)[:, None] >= slots) | (position > 0))
        table = jnp.where(keep[:, None], jnp.take(tm_bias[0], jnp.clip(offset, 0, window - 1), axis=1).transpose(1, 0, 2), MASKED)
        table = jnp.broadcast_to(table[:, None, :, :, None], (2 * slots, 8, heads, slots, 8)).reshape(2 * slots, 8, heads * slots * 8)
        swap = lambda a: jnp.swapaxes(a, 1, 2)
        vmem = pl.BlockSpec(memory_space=pltpu.VMEM)
        smem = pl.BlockSpec(memory_space=pltpu.SMEM)
        dma = pltpu.SemaphoreType.DMA
        fin_a, fin_b, emit_a, emit_b = pl.pallas_call(
            functools.partial(kernel, group, heads),
            in_specs=[vmem] * 6 + [smem] * 2 + [vmem] * 9,
            out_specs=[vmem] * 4,
            out_shape=[jax.ShapeDtypeStruct((slots, channels, tokens), F32)] * 2 + [jax.ShapeDtypeStruct((steps, tokens // group, channels), F32)] * 2,
            scratch_shapes=[
                pltpu.VMEM((2, slots + 1, tokens, channels), F32),
                pltpu.VMEM((2, tokens, channels), F32),
                pltpu.VMEM((2, steps, tokens, channels), F32),
                pltpu.VMEM((2, slots, 6, dim), F32),
                pltpu.SMEM((2, slots), F32),
                pltpu.VMEM((2, pairs, 2 * tokens, dim), BF16),
                pltpu.VMEM((2, 2 * pairs, 2 * tokens, dim), BF16),
                pltpu.VMEM((pairs, 2 * tokens, dim), BF16),
                pltpu.VMEM((2, steps, tokens // group, channels), F32),
                dma((2, pairs)), dma((2, pairs)), pltpu.SemaphoreType.REGULAR((2,)),
                dma((2,)), dma((2,)), dma((2, group)), dma((2, steps)),
            ],
            compiler_params=pltpu.CompilerParams(collective_id=0, has_side_effects=True, vmem_limit_bytes=62 * 1024 * 1024),
            name='queues',
        )(swap(latents_a), swap(latents_b), swap(noise_a), swap(noise_b), mod_a[:, 0], mod_b[:, 0], dt_a, dt_b, table, w_in,
          sp_t, sp_out[0].reshape(dim, dim), tm_t, tm_out[0].reshape(dim, dim), mlp_up[0].T, mlp_down[0].T, out_t)
        return emit_a, swap(fin_a), emit_b, swap(fin_b)

    return jax.shard_map(local, mesh=mesh, in_specs=(slot_spec, slot_spec, slot_spec, P('videos'), slot_spec, slot_spec, slot_spec, P('videos')) + (whole,) * 9, out_specs=(emit_spec, slot_spec, emit_spec, slot_spec), check_vma=False)
```

time: 643 us -> 453 us (0.70)
  waiting for transfers between devices: 68.8 us -> 0 us
  local copies, waits for them, and re-layouts: 52.4 us -> 14 us
  starting transfers between devices: 36.6 us -> 0 us
  Pallas kernels: 468 us -> 438 us
  between operations: 14.2 us -> 0.71 us
    unnamed x2 -> x0, waiting for transfers between devices: 62.9 us -> none
    ppermute x12 -> x0, starting transfers between devices: 36.6 us -> none  [the longest x6 28.7 us: step(): halos = [lax.ppermute(front[n][1], 'frames', to_next) for n in range(2)]]
    pallas_call x18 -> x1, Pallas kernels: 468 us -> 438 us  [local(): pl.pallas_call(functools.partial(kernel, group, heads), in_specs=[vmem] *...]
    slice x28 -> x0, local copies, waits for them, and re-layouts: 19.2 us -> none  [the longest x15 13.1 us: step(): new.append(jnp.concatenate([updated[1:], incoming[None]], axis=0))]
    while x12 -> x0, local copies, waits for them, and re-layouts: 12.1 us -> none
  transfers between devices with their start and end apart: 13 -> 0, of which waited for: 4 -> 0; matrix products, arithmetic and copies ran while one was open for 5% -> 0% of each run, Pallas kernels for 61% -> 0%
where the time goes in v2:
time: 453 us
  Pallas kernels  438 us (97%)
  local copies, waits for them, and re-layouts  14 us (3%)
    pallas_call x1, Pallas kernels, local(): pl.pallas_call(functools.partial(kernel, group, heads), in_specs=[vmem] *...  438 us

profile of v2, /device:TPU:22, one launch (start us, length us, event | category | flops | bytes accessed | tf_op | source)
XLA Modules:
  0.0 452.5 jit_solution(17294013739124140695)
XLA Ops:
  0.7 0.1 fusion.4
  0.7 0.8 copy.40
  1.5 1.3 pad.4.out_t
  2.8 0.1 reshape.122
  2.9 0.0 copy-start.2
  2.9 0.0 copy-start.3
  2.9 1.0 gather_fusion
  4.0 0.2 select_bitcast_fusion
  4.2 0.2 copy.30
  4.4 0.0 copy-start
  4.4 0.1 copy.31
  4.5 0.0 copy-done.2
  4.5 0.0 copy-done.3
  4.5 0.8 copy_bitcast_fusion
  5.3 0.9 broadcast_in_dim.42.table
  6.3 0.0 copy-done
  6.3 0.0 copy-start.1
  6.3 1.4 copy.32
  7.7 0.0 copy-done.1
  7.7 1.5 copy.33
  9.2 437.5 %queues.1 = (f32[16,4,256]{2,1,0:T(4,128)}, f32[16,4,256]{2,1,0:T(4,128)}, f32[3,16,4]{2,1,0:T(8,128)}, f32[3,16,4]{2,1,0:T(8,128)}) custom-call(f32[16,4,256]{2,1,0:T(4,128)} %bitcast.47, f32[16,4,256]{2,1,0:T(4,128)} %bitcast.48, f32[3,4,256]{2,1,0:T(4,128)} %bitcast.51, f32[3,4,256]{2,1,0:T(4,128)} %bitcast.52, f32[16,6,384]{2,1,0:T(8,128)} %get-tuple-element.23.mod_a, ...), custom_call_target="tpu_custom_call" | custom-call | tf_op jit(solution)/shard_map/queues/pallas_call | solution.py:350
  446.8 1.4 copy.36
  448.2 1.4 copy.37
  449.6 1.5 copy.45
  451.1 1.5 copy.46
  (5 shorter events, 0.1 us)
Async XLA Ops:
  2.9 1.6 copy-start.2
  2.9 1.6 copy-start.3
  4.4 1.9 copy-start
  6.3 1.4 copy-start.1
